TPU v7x, 128 devices: a whole 4x4x4 slice. The times are simulated.
128 devices in a mesh: gz: 32 (over y_lo, z, x), col: 4 (over y_hi, core).
Axes of the slice: x: 4, y: 4 (y_hi: 2, y_lo: 2; y = y_hi * 2 + y_lo), z: 4, core: 2. Of those that a mesh axis runs over, the one named last changes fastest.
Arguments:
- features: bfloat16 [64, 64, 128, 128], P(None, 'gz'), may hold values from -6 to 6
- grad_out: bfloat16 [64, 64, 128, 128], P('col', 'gz'), may hold values from -6 to 6
- conv_weight: bfloat16 [64, 64, 27], P('col'), may hold values from -0.15625 to 0.15625
- spectral_weight: bfloat16 [64, 64, 16, 256], P(None, 'col', None, 'gz'), may hold values from -3 to 3
Outputs:
- layer_out: bfloat16 [64, 64, 128, 128], P('col', 'gz')
- grad_input: bfloat16 [64, 64, 128, 128], P('col', 'gz')
- grad_conv: float32 [64, 64, 27], P('col')
- grad_spectral: float32 [64, 64, 16, 256], P(None, 'col', None, 'gz')
All inputs are finite; a program needn't handle non-finite values.
Results may differ from a plain program's by a relative error of at most 0.008.
Values may be sent and summed in bfloat16 or wider, within the bound.
No kernel may reach another device: no remote copies, remote signals or barrier semaphores. Data moves between devices by JAX's collectives and lax.ppermute only.
A program may use at most 256 MiB of HBM per device.

v0:
```python
from functools import partial
import math

import jax
import jax.numpy as jnp
from jax import lax
from jax.sharding import PartitionSpec as P

highest = lax.Precision.HIGHEST


def with_halo(block, sides, width):
    for axis, dim in sides:
        count = lax.axis_size(axis)
        forward = [(i, i + 1) for i in range(count - 1)]
        forward.append((count - 1, 0))
        backward = [(target, source) for source, target in forward]
        low = lax.ppermute(
            lax.slice_in_dim(block, block.shape[dim] - width, None, axis=dim), axis, forward
        )
        high = lax.ppermute(lax.slice_in_dim(block, 0, width, axis=dim), axis, backward)
        block = jnp.concatenate([low, block, high], axis=dim)
    return block


def laid_out(blocks, dim):
    lengths = list(blocks.shape[1:])
    lengths[dim] *= blocks.shape[0]
    return jnp.moveaxis(blocks, 0, dim).reshape(lengths)


def copy_for_each(value, axis):
    copies = jnp.broadcast_to(value, (lax.axis_size(axis), *value.shape))
    return lax.all_to_all(copies, axis, split_axis=0, concat_axis=0, tiled=True)


def gather_directly(value, axis, dim):
    return laid_out(copy_for_each(value, axis), dim)


def over_pieces(value, axis):
    blocks = lax.all_gather(value, axis)
    return blocks.sum(axis=0)


def split_up(value, dim, length):
    lengths = value.shape
    blocks = value.reshape(*lengths[:dim], length, lengths[dim] // length, *lengths[dim + 1 :])
    return jnp.moveaxis(blocks, dim, 0)


def sum_at_owner(value, axis, dim):
    length = lax.axis_size(axis)
    blocks = lax.all_to_all(split_up(value, dim, length), axis, 0, 0, tiled=True)
    return jnp.sum(blocks.astype(jnp.float32), axis=0)


def basis(length, mode_count):
    indices = jnp.arange(mode_count, dtype=jnp.int32)
    middle = mode_count // 2
    cosine_rows = indices <= middle
    frequency = jnp.where(cosine_rows, indices, indices - middle)
    positions = jnp.arange(length, dtype=jnp.int32)
    residue = frequency[:, None] * positions[None, :] % length
    radians = residue.astype(jnp.float32) * (2.0 * math.pi / length)
    tables = jnp.where(cosine_rows[:, None], jnp.cos(radians), jnp.sin(radians))
    return tables * math.sqrt(2.0 / length)


def activate(preact, cotangent):
    outcome, pullback = jax.vjp(partial(jax.nn.gelu, approximate=True), preact)
    return (outcome, pullback(cotangent)[0])


def wrap_pad(volume):
    return jnp.pad(volume, ((0, 0), (0, 0), (1, 1), (1, 1)), mode="wrap")


def correlate(padded, kernel):
    numbers = ("NCDHW", "OIDHW", "NCDHW")
    return lax.conv_general_dilated(
        padded[None],
        kernel,
        (1, 1, 1),
        "VALID",
        dimension_numbers=numbers,
        preferred_element_type=jnp.float32,
    )[0]


def analyse(volume, table_x, table_y, table_z):
    channel_count, plane_count, size_x, size_y = volume.shape
    mode_count = table_y.shape[0]
    along_y = jnp.dot(
        volume.reshape(channel_count * plane_count * size_x, size_y),
        table_y.astype(jnp.bfloat16).T,
        preferred_element_type=jnp.float32,
    )
    along_y = along_y.reshape(channel_count, plane_count, size_x, mode_count)
    planes = jnp.einsum("kx,czxl->czkl", table_x, along_y, precision=highest)
    planes = planes.reshape(channel_count, plane_count, mode_count * mode_count)
    return jnp.einsum(
        "jz,czm->cjm",
        table_z,
        lax.all_to_all(planes, "gz", split_axis=2, concat_axis=1, tiled=True),
        precision=highest,
    )


def synthesise(spectrum, table_x, table_y, table_z):
    mode_count = table_x.shape[0]
    columns = jnp.einsum("jz,cjm->czm", table_z, spectrum, precision=highest)
    slabs = lax.all_to_all(columns, "gz", split_axis=1, concat_axis=2, tiled=True)
    channel_count, plane_count, merged = slabs.shape
    blocks = slabs.reshape(channel_count, plane_count, mode_count, mode_count)
    along_x = jnp.einsum("kx,czkl->czxl", table_x, blocks, precision=highest)
    return jnp.einsum("czxl,ly->czxy", along_x, table_y, precision=highest)


def local(features, grad_out, conv_weight, spectral_weight):
    channel_count, plane_count, size_x, size_y = features.shape
    share_count = conv_weight.shape[0]
    mode_count = spectral_weight.shape[2]
    groups = lax.axis_size("gz")
    table_x = basis(size_x, mode_count)
    table_y = basis(size_y, mode_count)
    table_z = basis(plane_count * groups, mode_count)
    first_channel = lax.axis_index("col") * share_count
    own_features = lax.dynamic_slice_in_dim(features, first_channel, share_count, 0)
    rimmed = with_halo(features, (("gz", 1),), 1)
    padded = wrap_pad(rimmed)
    kernel = conv_weight.reshape(share_count, channel_count, 3, 3, 3)
    conv_part = correlate(padded, kernel)
    weights32 = spectral_weight.astype(jnp.float32)
    spectrum = analyse(own_features, table_x, table_y, table_z)
    spectrum_all = gather_directly(spectrum, "col", 0)
    mixed = jnp.sum(weights32 * spectrum_all[:, None], axis=0)
    preact = conv_part + synthesise(mixed, table_x, table_y, table_z)
    outcome, slope = activate(preact, grad_out.astype(jnp.float32))
    layer_out = outcome.astype(jnp.bfloat16)
    grad_pre = slope.astype(jnp.bfloat16)
    grad_framed = with_halo(grad_pre, (("gz", 1),), 1)
    flipped = jnp.transpose(kernel, (1, 0, 2, 3, 4))[:, :, ::-1, ::-1, ::-1]
    contributions = correlate(wrap_pad(grad_framed), flipped)
    back_conv = lax.psum_scatter(contributions, "col", scatter_dimension=0, tiled=True)
    numbers = ("NCDHW", "OIDHW", "NCDHW")
    local_grad = lax.conv_general_dilated(
        padded[:, None],
        grad_pre[:, None],
        (1, 1, 1),
        "VALID",
        dimension_numbers=numbers,
        preferred_element_type=jnp.float32,
    )
    local_grad = jnp.transpose(local_grad, (1, 0, 2, 3, 4)).reshape(share_count, channel_count, 27)
    scaling = 1.0 / math.sqrt(size_x * size_y * plane_count * groups)
    grad_conv = over_pieces(local_grad, "gz") * scaling
    grad_modes = analyse(grad_pre, table_x, table_y, table_z)
    back_terms = jnp.sum(weights32 * grad_modes[None], axis=1)
    back_modes = sum_at_owner(back_terms.astype(jnp.bfloat16), "col", 0)
    grad_input = (back_conv + synthesise(back_modes, table_x, table_y, table_z)).astype(
        jnp.bfloat16
    )
    grad_spectral = spectrum_all[:, None] * grad_modes[None]
    return (layer_out, grad_input, grad_conv, grad_spectral)


def solution(mesh):
    return jax.shard_map(
        local,
        mesh=mesh,
        in_specs=(
            P(None, "gz", None, None),
            P("col", "gz", None, None),
            P("col", None, None),
            P(None, "col", None, "gz"),
        ),
        out_specs=(
            P("col", "gz", None, None),
            P("col", "gz", None, None),
            P("col", None, None),
            P(None, "col", None, "gz"),
        ),
        check_vma=False,
    )
```

profile of v0, /device:TPU:1, one launch (start us, length us, event | category | flops | bytes accessed | tf_op | source)
XLA Modules:
  0.0 872.3 jit_solution(11663966401610304900)
XLA Ops:
  8.1 6.7 copy.156
  14.7 5.1 fusion.136
  19.8 7.8 collective-permute-start.1
  27.7 1.7 fusion.36
  30.6 48.1 %all_to_all.76 = f32[32,1,256]{2,1,0:T(1,128)S(1)} all-to-all(f32[32,1,256]{2,1,0:T(1,128)S(1)} %reshape.81), channel_id=1, replica_groups=mesh['gz'=32,'col'=4] {'gz'}, dimensions={0} | all-to-all | bytes 65536 | tf_op jit(solution)/shard_map/all_to_all | solution.py:105
  81.3 10.5 %all_to_all.77 = f32[4,1,2048]{2,1,0:T(1,128)S(1)} all-to-all(f32[4,1,2048]{2,1,0:T(1,128)S(1)} %reshape.83), channel_id=1, replica_groups=mesh['gz'=32,'col'=4] {'col'}, dimensions={0} | all-to-all | bytes 65536 | tf_op jit(solution)/shard_map/all_to_all | solution.py:34
  91.8 0.7 reduce.1
  94.1 10.3 %all_to_all.78 = f32[32,1,256]{2,1,0:T(1,128)S(1)} all-to-all(f32[32,1,256]{2,1,0:T(1,128)S(1)} %reshape.85), channel_id=1, replica_groups=mesh['gz'=32,'col'=4] {'gz'}, dimensions={0} | all-to-all | bytes 65536 | tf_op jit(solution)/shard_map/all_to_all | solution.py:113
  104.4 0.7 reduce.2
  106.1 3.8 pad_maximum_fusion.8
  109.9 7.0 fusion.135
  116.9 42.4 %fusion.153 = bf16[64,4,130,1,130]{2,0,4,1,3:T(8,128)(2,1)} fusion(bf16[64,4,1,128]{2,0,3,1:T(8,128)(2,1)} %get-tuple-element.5, bf16[64,1,128,128]{2,0,3,1:T(8,128)(2,1)S(1)} %collective-permute-done.1, bf16[64,2,128,128]{2,0,3,1:T(8,128)(2,1)} %copy.156, bf16[64,1,128,128]{2,0,3,1:T(8,128)(2,1)} %collective-permute-done, ...), kind=kLoop, calls=%fused_computation.184 | loop fusion | flops 129792000 | bytes 17172480 | tf_op jit(solution)/shard_map/broadcast_in_dim | solution.py:82
  159.3 15.7 %pad = bf16[64,4,130,1,136]{2,0,4,1,3:T(8,128)(2,1)} pad(bf16[64,4,130,1,130]{2,0,4,1,3:T(8,128)(2,1)} %fusion.153, bf16[]{:T(256)} %constant.70), padding=0_0x0_0x0_0x0_0x0_6 | pad | bytes 17704962 | tf_op jit(solution)/shard_map/broadcast_in_dim | solution.py:82
  175.0 29.9 %copy.160 = bf16[64,4,130,1,8,17]{0,4,5,2,1,3:T(8,128)(2,1)} copy(bf16[64,4,130,1,8,17]{2,0,5,4,1,3:T(8,128)(2,1)} %bitcast.135) | data formatting | bytes 18104320 | tf_op jit(solution)/shard_map/conv_general_dilated | solution.py:81
  204.9 2.2 slice.64
  207.1 71.5 %broadcast_select_fusion.1 = f32[2,128,8,17,16]{4,2,3,1,0:T(8,128)} fusion(pred[8,17]{0,1:T(8,128)(4,1)S(1)} %copy-done.9, bf16[16,64,3,3,3]{1,0,4,3,2:T(8,128)(2,1)S(1)} %bitcast.133, bf16[64,4,130,1,7,2]{0,4,5,2,1,3:T(8,128)(2,1)S(1)} %slice.64, bf16[64,4,130,1,8,17]{0,4,5,2,1,3:T(8,128)(2,1)} %copy.160), kind=kOutput, calls=%fused_computation.29 | convolution fusion | flops 1956093952 | bytes 12267656 | tf_op jit(solution)/shard_map/conv_general_dilated | solution.py:81
  278.6 11.9 %copy.161 = f32[2,128,8,17,16]{1,4,3,2,0:T(8,128)} copy(f32[2,128,8,17,16]{4,2,3,1,0:T(8,128)} %broadcast_select_fusion.1) | data formatting | bytes 4456448 | tf_op jit(solution)/shard_map/conv_general_dilated | solution.py:81
  290.4 3.0 slice.65
  293.5 3.0 copy.202
  296.4 7.0 fusion.26
  303.5 1.0 fusion.138
  304.5 1.7 collective-permute-start.3
  306.2 42.4 %fusion.152 = bf16[64,1,4,130,130]{3,0,4,2,1:T(8,128)(2,1)} fusion(bf16[64,4,1,128]{2,0,3,1:T(8,128)(2,1)} %get-tuple-element.5, bf16[64,1,128,128]{2,0,3,1:T(8,128)(2,1)S(1)} %collective-permute-done.1, bf16[64,2,128,128]{2,0,3,1:T(8,128)(2,1)} %copy.156, bf16[64,1,128,128]{2,0,3,1:T(8,128)(2,1)} %collective-permute-done, ...), kind=kLoop, calls=%fused_computation.183 | loop fusion | flops 129792000 | bytes 17172480 | tf_op jit(solution)/shard_map/broadcast_in_dim | solution.py:148
  348.6 70.9 %copy.191 = bf16[64,1,4,130,130]{0,1,4,3,2:T(2,128)(2,1)} copy(bf16[64,1,4,130,130]{3,0,4,2,1:T(8,128)(2,1)} %fusion.152) | data formatting | bytes 17305600 | tf_op jit(solution)/shard_map/broadcast_in_dim | solution.py:148
  419.5 17.7 %copy.192 = bf16[16,1,2,128,128]{0,1,4,3,2:T(2,128)(2,1)} copy(bf16[16,1,2,128,128]{4,3,2,0,1:T(8,128)(2,1)S(1)} %bitcast.136) | data formatting | bytes 2097152 | tf_op jit(solution)/shard_map/broadcast_in_dim | solution.py:149
  437.2 233.7 %fusion.139 = f32[16,64,3,3,3]{1,0,4,3,2:T(8,128)} fusion(bf16[64,1,4,130,130]{0,1,4,3,2:T(2,128)(2,1)} %copy.191, bf16[16,1,2,128,128]{0,1,4,3,2:T(2,128)(2,1)} %copy.192), kind=kOutput, calls=%fused_computation.182 | convolution fusion | flops 1811939328 | bytes 9811968 | tf_op jit(solution)/shard_map/transpose | solution.py:155
  671.0 0.9 pad_maximum_fusion.12
  671.8 2.6 pad_maximum_fusion.9
  674.5 0.8 fusion.137
  675.3 7.7 maximum_bitcast_fusion
  683.0 8.3 copy.204
  691.3 5.2 pad.2.clone
  696.5 18.3 %copy.176 = bf16[16,4,130,1,8,17]{0,4,5,2,1,3:T(8,128)(2,1)} copy(bf16[16,4,130,1,8,17]{2,0,5,4,1,3:T(8,128)(2,1)} %bitcast.139) | data formatting | bytes 4526080 | tf_op jit(solution)/shard_map/conv_general_dilated | solution.py:81
  714.7 2.2 slice.70
  716.9 29.9 %broadcast_select_fusion = f32[2,128,8,17,64]{4,2,3,1,0:T(8,128)} fusion(pred[8,17]{0,1:T(8,128)(4,1)S(1)} %copy-done.10, bf16[16,64,3,3,3]{1,0,4,3,2:T(8,128)(2,1)S(1)} %bitcast.134, bf16[16,4,130,1,7,2]{0,4,5,2,1,3:T(8,128)(2,1)S(1)} %slice.70, bf16[16,4,130,1,8,17]{0,4,5,2,1,3:T(8,128)(2,1)} %copy.176), kind=kOutput, calls=%fused_computation.28 | convolution fusion | flops 1935001600 | bytes 11464328 | tf_op jit(solution)/shard_map/conv_general_dilated | solution.py:81
  746.8 15.0 %copy.177 = f32[2,128,8,17,64]{1,4,3,2,0:T(8,128)} copy(f32[2,128,8,17,64]{4,2,3,1,0:T(8,128)} %broadcast_select_fusion) | data formatting | bytes 17825792 | tf_op jit(solution)/shard_map/conv_general_dilated | solution.py:81
  761.8 8.3 slice.71
  770.1 9.3 %copy.203 = f32[2,128,1,128,64]{3,1,0,4,2:T(8,128)} copy(f32[2,128,1,128,64]{1,4,3,2,0:T(8,128)} %slice.71) | data formatting | bytes 16777216
  781.2 14.3 %all_to_all.79 = f32[32,1,256]{2,1,0:T(1,128)S(1)} all-to-all(f32[32,1,256]{2,1,0:T(1,128)S(1)} %reshape.87), channel_id=1, replica_groups=mesh['gz'=32,'col'=4] {'gz'}, dimensions={0} | all-to-all | bytes 65536 | tf_op jit(solution)/shard_map/all_to_all | solution.py:105
  795.5 0.7 reduce.3
  797.4 1.3 broadcast_multiply_fusion
  799.0 11.3 %all_to_all.80 = bf16[4,2,1024]{2,1,0:T(2,128)(2,1)S(1)} all-to-all(bf16[4,2,1024]{2,1,0:T(2,128)(2,1)S(1)} %reshape.89), channel_id=1, replica_groups=mesh['gz'=32,'col'=4] {'col'}, dimensions={0} | all-to-all | bytes 32768 | tf_op jit(solution)/shard_map/all_to_all | solution.py:54
  811.1 10.3 %all_to_all.81 = f32[32,1,256]{2,1,0:T(1,128)S(1)} all-to-all(f32[32,1,256]{2,1,0:T(1,128)S(1)} %reshape.91), channel_id=1, replica_groups=mesh['gz'=32,'col'=4] {'gz'}, dimensions={0} | all-to-all | bytes 65536 | tf_op jit(solution)/shard_map/all_to_all | solution.py:113
  821.4 0.7 reduce.4
  823.1 3.7 reduce_sum.39
  826.8 0.7 broadcast_multiply_fusion.1
  827.5 31.4 %reduce-scatter.2.cloned.1.call-done = f32[16,2,128,128]{3,2,1,0:T(8,128)} async-done(((f32[64,2,128,128]{3,2,1,0:T(8,128)}), f32[16,2,128,128]{3,2,1,0:T(8,128)}) %reduce-scatter.2.cloned.1.call-update) | async-done | bytes 2097168 | tf_op jit(solution)/shard_map/reduce_scatter | solution.py:145
  858.9 5.7 add_convert_fusion
  (79 shorter events, 11.2 us)
Async XLA Ops:
  8.0 199.1 %copy-start = (bf16[16,64,27]{1,0,2:T(8,128)(2,1)S(1)}, bf16[16,64,27]{1,0,2:T(8,128)(2,1)}, u32[]{:S(2)}) copy-start(bf16[16,64,27]{1,0,2:T(8,128)(2,1)} %param.6) | copy-start | bytes 165892
  8.0 85.0 %copy-start.1 = (bf16[64,16,16,8]{0,3,2,1:T(8,128)(2,1)S(1)}, bf16[64,16,16,8]{0,3,2,1:T(8,128)(2,1)}, u32[]{:S(2)}) copy-start(bf16[64,16,16,8]{0,3,2,1:T(8,128)(2,1)} %param.7) | copy-start | bytes 786436
  8.0 815.1 %all-gather.2.cloned.1.call-start = ((), (), s32[]{:S(2)}) async-start(), calls=%async_computation.8 | async-start | bytes 7299072 | tf_op jit(solution)/shard_map/all_gather | solution.py:42
  19.8 86.2 %collective-permute-start.1 = (bf16[64,1,128,128]{2,0,3,1:T(8,128)(2,1)}, bf16[64,1,128,128]{2,0,3,1:T(8,128)(2,1)S(1)}, u32[]{:S(2)}, u32[]{:S(2)}) collective-permute-start(bf16[64,1,128,128]{2,0,3,1:T(8,128)(2,1)} %get-tuple-element.7), channel_id=1, source_target_pairs={{4,0},{8,4},{12,8},{16,12},{20,16},{24,20},{28,24},{32,28},{36,32}... | collective-permute-start | bytes 6291464 | tf_op jit(solution)/shard_map/ppermute | solution.py:21
  27.6 78.4 %collective-permute-start = (bf16[64,1,128,128]{2,0,3,1:T(8,128)(2,1)}, bf16[64,1,128,128]{2,0,3,1:T(8,128)(2,1)}, u32[]{:S(2)}, u32[]{:S(2)}) collective-permute-start(bf16[64,1,128,128]{2,0,3,1:T(8,128)(2,1)} %get-tuple-element.6), channel_id=1, source_target_pairs={{0,4},{4,8},{8,12},{12,16},{16,20},{20,24},{24,28},{28,32},{32,36}... | collective-permute-start | bytes 6291464 | tf_op jit(solution)/shard_map/ppermute | solution.py:18
  27.6 268.8 %copy-start.5 = (s32[16]{0:T(128)}, s32[16]{0:T(128)S(1)}, u32[]{:S(2)}) copy-start(s32[16]{0:T(128)S(1)} %add_select_fusion.2) | copy-start | bytes 196
  27.6 268.8 %copy-start.7 = (pred[16]{0:T(512)(128)(4,1)}, pred[16]{0:T(512)(128)(4,1)S(1)}, u32[]{:S(2)}) copy-start(pred[16]{0:T(512)(128)(4,1)S(1)} %iota_compare_fusion.2) | copy-start | bytes 52
  93.0 23.9 %copy-start.3 = (f32[64,16,8]{0,2,1:T(8,128)}, f32[64,16,8]{0,2,1:T(8,128)S(1)}, u32[]{:S(2)}) copy-start(f32[64,16,8]{0,2,1:T(8,128)S(1)} %mul.246) | copy-start | bytes 98308
  175.0 32.1 %copy-start.9 = (pred[8,17]{0,1:T(8,128)(4,1)S(1)}, pred[8,17]{0,1:T(8,128)(4,1)}, u32[]{:S(2)}) copy-start(pred[8,17]{0,1:T(8,128)(4,1)} %constant.78) | copy-start | bytes 412
  304.5 366.4 %collective-permute-start.3 = (bf16[16,1,128,128]{3,2,1,0:T(8,128)(2,1)}, bf16[16,1,128,128]{3,2,1,0:T(8,128)(2,1)}, u32[]{:S(2)}, u32[]{:S(2)}) collective-permute-start(bf16[16,1,128,128]{3,2,1,0:T(8,128)(2,1)} %get-tuple-element.15), channel_id=1, source_target_pairs={{4,0},{8,4},{12,8},{16,12},{20,16},{24,20},{28,24},{32,28},{36,32}... | collective-permute-start | bytes 1572872 | tf_op jit(solution)/shard_map/ppermute | solution.py:21
  306.2 364.8 %collective-permute-start.2 = (bf16[16,1,128,128]{3,2,1,0:T(8,128)(2,1)}, bf16[16,1,128,128]{3,2,1,0:T(8,128)(2,1)}, u32[]{:S(2)}, u32[]{:S(2)}) collective-permute-start(bf16[16,1,128,128]{3,2,1,0:T(8,128)(2,1)} %get-tuple-element.14), channel_id=1, source_target_pairs={{0,4},{4,8},{8,12},{12,16},{16,20},{20,24},{24,28},{28,32},{32,36}... | collective-permute-start | bytes 1572872 | tf_op jit(solution)/shard_map/ppermute | solution.py:18
  670.9 188.0 %reduce-scatter.2.cloned.1.call-start = ((), (), s32[]{:S(2)}) async-start(), calls=%async_computation.7 | async-start | bytes 10485760 | tf_op jit(solution)/shard_map/reduce_scatter | solution.py:145
  691.3 25.7 %copy-start.10 = (pred[8,17]{0,1:T(8,128)(4,1)S(1)}, pred[8,17]{0,1:T(8,128)(4,1)}, u32[]{:S(2)}) copy-start(pred[8,17]{0,1:T(8,128)(4,1)} %constant.78) | copy-start | bytes 412
  770.1 9.3 %copy-start.6 = (s32[16]{0:T(128)S(1)}, s32[16]{0:T(128)}, u32[]{:S(2)}) copy-start(s32[16]{0:T(128)} %copy-done.5) | copy-start | bytes 196
  770.1 9.4 %copy-start.8 = (pred[16]{0:T(512)(128)(4,1)S(1)}, pred[16]{0:T(512)(128)(4,1)}, u32[]{:S(2)}) copy-start(pred[16]{0:T(512)(128)(4,1)} %copy-done.7) | copy-start | bytes 52
  770.1 27.3 %copy-start.2 = (bf16[64,16,16,8]{0,3,2,1:T(8,128)(2,1)S(1)}, bf16[64,16,16,8]{0,3,2,1:T(8,128)(2,1)}, u32[]{:S(2)}) copy-start(bf16[64,16,16,8]{0,3,2,1:T(8,128)(2,1)} %param.7) | copy-start | bytes 786436
  770.1 27.3 %copy-start.4 = (f32[64,16,8]{0,2,1:T(8,128)S(1)}, f32[64,16,8]{0,2,1:T(8,128)}, u32[]{:S(2)}) copy-start(f32[64,16,8]{0,2,1:T(8,128)} %copy-done.3) | copy-start | bytes 98308
Sparse Core Ops, SparseCore 0:
  671.0 144.7 all-gather.1
Sparse Core Ops, SparseCore 1:
  779.5 79.3 reduce-scatter.1
where the time goes:
time: 888 us; the launch traced here: 872 us
  matrix products  354 us (40%)
  local copies, waits for them, and re-layouts  247 us (28%)
  other arithmetic  109 us (12%)
  blocking collectives  105 us (12%)
  waiting for transfers between devices  31.4 us (4%)
  between operations  16.2 us (2%)
  starting transfers between devices  9.52 us (1%)
    transpose x1, matrix products, local(): jnp.transpose(local_grad, (1, 0, 2, 3, 4))  234 us
    conv_general_dilated x2, matrix products, correlate(): lax.conv_general_dilated(padded[None], kernel, (1, 1, 1), 'VALID', dimens...  101 us
    conv_general_dilated x8, local copies, waits for them, and re-layouts, correlate(): lax.conv_general_dilated(padded[None], kernel, (1, 1, 1), 'VALID', dimens...  90.7 us
    broadcast_in_dim x1, local copies, waits for them, and re-layouts, local(): padded[:, None]  70.9 us
    all_to_all x2, blocking collectives, analyse(): lax.all_to_all(planes, 'gz', split_axis=2, concat_axis=1, tiled=True)  62.4 us
    broadcast_in_dim x2, other arithmetic, correlate(): padded[None]  50.1 us
    broadcast_in_dim x1, other arithmetic, local(): padded[:, None]  42.4 us
    reduce_scatter x1, waiting for transfers between devices, local(): lax.psum_scatter(contributions, 'col', scatter_dimension=0, tiled=True)  31.4 us
  transfers between devices with their start and end apart: 6, of which 1 were waited for; matrix products, arithmetic and copies ran while one was open for 57% of the time, Pallas kernels for 0%

commit v1 on v0

v1 whole, which is shorter than its diff:
```python
import math

import jax
import jax.numpy as jnp
from jax import lax
from jax.experimental import pallas as pl
from jax.experimental.pallas import tpu as pltpu
from jax.sharding import PartitionSpec as P

highest = lax.Precision.HIGHEST
f32 = jnp.float32
bf16 = jnp.bfloat16
SIDE = 128
OWN = 16
ALL = 64
UNROLL = 8
GELU_A = math.sqrt(2.0 / math.pi)
GELU_B = 0.044715

PLANE_TERMS = (((0, 2),), ((0, 1), (1, 2)), ((0, 0), (1, 1)), ((1, 0),))


def basis(length, mode_count):
    indices = jnp.arange(mode_count, dtype=jnp.int32)
    middle = mode_count // 2
    cosine_rows = indices <= middle
    frequency = jnp.where(cosine_rows, indices, indices - middle)
    positions = jnp.arange(length, dtype=jnp.int32)
    residue = frequency[:, None] * positions[None, :] % length
    radians = residue.astype(jnp.float32) * (2.0 * math.pi / length)
    tables = jnp.where(cosine_rows[:, None], jnp.cos(radians), jnp.sin(radians))
    return tables * math.sqrt(2.0 / length)


def split2(value):
    high = value.astype(bf16)
    low = (value - high.astype(f32)).astype(bf16)
    return high, low


def dot(a, b):
    return jnp.dot(a, b, preferred_element_type=f32)


def dot_nt(a, b):
    return lax.dot_general(a, b, (((1,), (1,)), ((), ())), preferred_element_type=f32)


def conv_rows(slab, w_ref, int_ref, rim_ref):
    def block(step, carry):
        w = w_ref[...]
        for u in range(UNROLL):
            x = step * UNROLL + u
            near = ((x + SIDE - 1) % SIDE, x, (x + 1) % SIDE)
            rhs = jnp.concatenate(
                [jnp.concatenate([slab(z, n) for n in near], axis=0) for z in range(2)], axis=1
            )
            r = dot(w, rhs)

            def part(z, a, c):
                row = (a * 3 + c) * OWN
                return r[row : row + OWN, z * SIDE : (z + 1) * SIDE]

            for plane, terms in enumerate(PLANE_TERMS):
                c0, c1, c2 = (sum(part(z, a, c) for z, a in terms) for c in range(3))
                total = c1 + pltpu.roll(c0, 1, axis=1) + pltpu.roll(c2, SIDE - 1, axis=1)
                if plane in (1, 2):
                    int_ref[pl.ds((plane - 1) * SIDE + x, OWN, stride=2 * SIDE), :] = total
                else:
                    rim_ref[pl.ds((plane // 3) * SIDE + x, OWN, stride=2 * SIDE), :] = total
        return carry

    lax.fori_loop(0, SIDE // UNROLL, block, 0)


def write_rims(rim_ref, low_ref, high_ref):
    def block(o, carry):
        low_ref[o] = rim_ref[pl.ds(o * 2 * SIDE, SIDE), :].astype(bf16)
        high_ref[o] = rim_ref[pl.ds(o * 2 * SIDE + SIDE, SIDE), :].astype(bf16)
        return carry

    lax.fori_loop(0, OWN, block, 0)


def forward_conv_kernel(f_ref, w_ref, xt_ref, int_ref, low_ref, high_ref, rim_ref, turn_ref):
    def turn(step, carry):
        for z in range(2):
            rows = f_ref[:, z, pl.ds(step * 16, 16), :].astype(f32)
            turn_ref[z] = rows.reshape(ALL * 16, SIDE)
        for z in range(2):
            for u in range(16):
                xt_ref[z, step * 16 + u] = turn_ref[z, pl.ds(u, ALL, stride=16), :].astype(bf16)
        return carry

    lax.fori_loop(0, SIDE // 16, turn, 0)
    conv_rows(lambda z, x: xt_ref[z, x], w_ref, int_ref, rim_ref)
    write_rims(rim_ref, low_ref, high_ref)


def forward_conv(features, w):
    return pl.pallas_call(
        forward_conv_kernel,
        out_shape=(
            jax.ShapeDtypeStruct((2, SIDE, ALL, SIDE), bf16),
            jax.ShapeDtypeStruct((OWN * 2 * SIDE, SIDE), f32),
            jax.ShapeDtypeStruct((OWN, SIDE, SIDE), bf16),
            jax.ShapeDtypeStruct((OWN, SIDE, SIDE), bf16),
        ),
        scratch_shapes=[
            pltpu.VMEM((OWN * 2 * SIDE, SIDE), f32),
            pltpu.VMEM((2, ALL * 16, SIDE), f32),
        ],
        name="forward_conv",
    )(features, w)


def back_conv_kernel(g0, g1, g2, g3, w_ref, int_ref, low_ref, high_ref, rim_ref):
    def slab(z, x):
        return jnp.concatenate([g[z, x] for g in (g0, g1, g2, g3)], axis=0)

    conv_rows(slab, w_ref, int_ref, rim_ref)
    write_rims(rim_ref, low_ref, high_ref)


def back_conv(shares, w):
    return pl.pallas_call(
        back_conv_kernel,
        out_shape=(
            jax.ShapeDtypeStruct((OWN * 2 * SIDE, SIDE), f32),
            jax.ShapeDtypeStruct((OWN, SIDE, SIDE), bf16),
            jax.ShapeDtypeStruct((OWN, SIDE, SIDE), bf16),
        ),
        scratch_shapes=[pltpu.VMEM((OWN * 2 * SIDE, SIDE), f32)],
        name="back_conv",
    )(*shares, w)


def finish_modes(g_ref, ey2, out_ref, width):
    for kx in range(16):
        high, low = split2(g_ref[kx * width : (kx + 1) * width, :])
        out_ref[kx * 16 : (kx + 1) * 16, :] = dot_nt(ey2, jnp.concatenate([high, low], axis=1))


def analyse_kernel(f_ref, ex2_ref, ey2_ref, out_ref, g_ref):
    def block(step, carry):
        ex2 = ex2_ref[...]
        for u in range(8):
            ch = step * 8 + u
            r = dot(ex2, jnp.concatenate([f_ref[ch, 0], f_ref[ch, 1]], axis=1))
            g = r[:16] + r[16:]
            g_ref[pl.ds(ch, 16, stride=2 * ALL), :] = g[:, :SIDE]
            g_ref[pl.ds(ch + ALL, 16, stride=2 * ALL), :] = g[:, SIDE:]
        return carry

    lax.fori_loop(0, ALL // 8, block, 0)
    finish_modes(g_ref, ey2_ref[...], out_ref, 2 * ALL)


def analyse(features, ex2, ey2):
    return pl.pallas_call(
        analyse_kernel,
        out_shape=jax.ShapeDtypeStruct((256, 2 * ALL), f32),
        scratch_shapes=[pltpu.VMEM((16 * 2 * ALL, SIDE), f32)],
        name="analyse",
    )(features, ex2, ey2)


def along_y(s_ref, eyh_ref, eyl_ref, t_ref):
    high, low = split2(s_ref[...])
    eyh = eyh_ref[...]
    t_ref[...] = dot(high, eyh) + dot(low, eyh) + dot(high, eyl_ref[...])


def along_x(t_ref, ext3, o):
    t = jnp.concatenate([t_ref[pl.ds(o * 32, 16), :], t_ref[pl.ds(o * 32 + 16, 16), :]], axis=1)
    high, low = split2(t)
    return dot(ext3, jnp.concatenate([high, high, low], axis=0))


def middle_kernel(
    int_ref, fl_ref, fh_ref, s_ref, go_ref, ex2_ref, ey2_ref, ext3_ref, eyh_ref, eyl_ref,
    out_ref, gt_ref, modes_ref, t_ref, g_ref, turn_ref,
):
    along_y(s_ref, eyh_ref, eyl_ref, t_ref)

    def block(o, carry):
        smooth = along_x(t_ref, ext3_ref[...], o)
        halves = []
        for z in range(2):
            rim = (fl_ref if z == 0 else fh_ref)[o].astype(f32)
            p = int_ref[pl.ds(o * 256 + z * SIDE, SIDE), :] + rim + smooth[:, z * SIDE : (z + 1) * SIDE]
            square = p * p
            t = jnp.tanh(GELU_A * p * (1.0 + GELU_B * square))
            half = 0.5 * (1.0 + t)
            out_ref[o, z] = (p * half).astype(bf16)
            slope = half + 0.5 * p * (1.0 - t * t) * (GELU_A * (1.0 + 3.0 * GELU_B * square))
            g = (go_ref[o, z].astype(f32) * slope).astype(bf16)
            halves.append(g)
            turn_ref[pl.ds(o * 256 + z * SIDE, SIDE), :] = g.astype(f32)
        r = dot(ex2_ref[...], jnp.concatenate(halves, axis=1))
        r = r[:16] + r[16:]
        g_ref[pl.ds(o, 16, stride=2 * OWN), :] = r[:, :SIDE]
        g_ref[pl.ds(o + OWN, 16, stride=2 * OWN), :] = r[:, SIDE:]
        return carry

    lax.fori_loop(0, OWN, block, 0)
    finish_modes(g_ref, ey2_ref[...], modes_ref, 2 * OWN)

    def turn(step, carry):
        for z in range(2):
            for u in range(UNROLL):
                x = step * UNROLL + u
                gt_ref[z, x] = turn_ref[pl.ds(z * SIDE + x, OWN, stride=2 * SIDE), :].astype(bf16)
        return carry

    lax.fori_loop(0, SIDE // UNROLL, turn, 0)


def middle(conv_int, from_low, from_high, slab, grad_out, tables):
    ex2, ey2, ext3, eyh, eyl = tables
    return pl.pallas_call(
        middle_kernel,
        out_shape=(
            jax.ShapeDtypeStruct((OWN, 2, SIDE, SIDE), bf16),
            jax.ShapeDtypeStruct((2, SIDE, OWN, SIDE), bf16),
            jax.ShapeDtypeStruct((256, 2 * OWN), f32),
        ),
        scratch_shapes=[
            pltpu.VMEM((OWN * 2 * 16, SIDE), f32),
            pltpu.VMEM((16 * 2 * OWN, SIDE), f32),
            pltpu.VMEM((OWN * 2 * SIDE, SIDE), f32),
        ],
        name="middle",
    )(conv_int, from_low, from_high, slab, grad_out, ex2, ey2, ext3, eyh, eyl)


def kernel_grad_kernel(xt_ref, gt_ref, gl_ref, gh_ref, out_ref):
    out_ref[...] = jnp.zeros_like(out_ref)

    def block(step, carry):
        lefts, rights = [], []
        for u in range(UNROLL):
            x = step * UNROLL + u
            near = ((x + SIDE - 1) % SIDE, x, (x + 1) % SIDE)
            for z in range(2):
                lefts.append(jnp.concatenate([xt_ref[z, n] for n in near], axis=0))
            planes = []
            for g in (gl_ref[x], gt_ref[0, x], gt_ref[1, x], gh_ref[x]):
                wide = g.astype(f32)
                planes.append((
                    pltpu.roll(wide, SIDE - 1, axis=1).astype(bf16),
                    g,
                    pltpu.roll(wide, 1, axis=1).astype(bf16),
                ))
            for z in range(2):
                rights.append(jnp.concatenate([planes[z - a + 2][c] for a in range(3) for c in range(3)], axis=0))
        out_ref[...] += dot_nt(jnp.concatenate(lefts, axis=1), jnp.concatenate(rights, axis=1))
        return carry

    lax.fori_loop(0, SIDE // UNROLL, block, 0)


def kernel_grad(xt, gt, gl, gh):
    return pl.pallas_call(
        kernel_grad_kernel,
        out_shape=jax.ShapeDtypeStruct((3 * ALL, 9 * OWN), f32),
        name="kernel_grad",
    )(xt, gt, gl, gh)


def last_kernel(int_ref, fl_ref, fh_ref, s_ref, ext3_ref, eyh_ref, eyl_ref, out_ref, t_ref):
    along_y(s_ref, eyh_ref, eyl_ref, t_ref)

    def block(o, carry):
        smooth = along_x(t_ref, ext3_ref[...], o)
        for z in range(2):
            rim = (fl_ref if z == 0 else fh_ref)[o].astype(f32)
            p = int_ref[pl.ds(o * 256 + z * SIDE, SIDE), :] + rim + smooth[:, z * SIDE : (z + 1) * SIDE]
            out_ref[o, z] = p.astype(bf16)
        return carry

    lax.fori_loop(0, OWN, block, 0)


def last(conv_int, from_low, from_high, slab, tables):
    _, _, ext3, eyh, eyl = tables
    return pl.pallas_call(
        last_kernel,
        out_shape=jax.ShapeDtypeStruct((OWN, 2, SIDE, SIDE), bf16),
        scratch_shapes=[pltpu.VMEM((OWN * 2 * 16, SIDE), f32)],
        name="last",
    )(conv_int, from_low, from_high, slab, ext3, eyh, eyl)


def ring(axis, step):
    count = lax.axis_size(axis)
    return [(i, (i + step) % count) for i in range(count)]


def swap(value, bits):
    count = lax.axis_size("col")
    return lax.ppermute(value, "col", [(i, i ^ bits) for i in range(count)])


def to_slabs(mixed, table_z):
    columns = jnp.einsum("jz,cjm->czm", table_z, mixed, precision=highest)
    slabs = lax.all_to_all(columns, "gz", split_axis=1, concat_axis=2, tiled=True)
    return slabs.reshape(OWN * 2 * 16, 16)


def sum_over_slabs(value):
    def stage(value, period, stride):
        count = lax.axis_size("gz")
        total = value
        for k in range(1, period):
            pairs = []
            for i in range(count):
                digit = i // stride % period
                pairs.append((i, i + ((digit + k) % period - digit) * stride))
            total = total + lax.ppermute(value, "gz", pairs)
        return total

    return stage(stage(stage(value, 4, 1), 4, 4), 2, 16)


def local(features, grad_out, conv_weight, spectral_weight):
    plane_count = features.shape[1]
    groups = lax.axis_size("gz")
    table_x = basis(SIDE, 16)
    table_y = basis(SIDE, 16)
    table_z = basis(plane_count * groups, 16)
    exh, exl = split2(table_x)
    eyh, eyl = split2(table_y)
    ex2 = jnp.concatenate([exh, exl], axis=0)
    ey2 = jnp.concatenate([eyh, eyh], axis=1)
    ext3 = jnp.concatenate([exh.T, exl.T, exh.T], axis=1)
    tables = (ex2, ey2, ext3, eyh, eyl)
    first = lax.axis_index("col") * OWN

    kernel = conv_weight.reshape(OWN, ALL, 3, 3, 3)
    w_forward = jnp.transpose(kernel, (2, 4, 0, 3, 1)).reshape(9 * OWN, 3 * ALL)
    pieces = []
    for bits in range(4):
        there = jnp.bitwise_xor(lax.axis_index("col"), bits) * OWN
        piece = lax.dynamic_slice_in_dim(conv_weight, there, OWN, 1)
        pieces.append(swap(piece, bits) if bits else piece)
    back = jnp.stack(pieces).reshape(4, OWN, OWN, 3, 3, 3)[:, :, :, ::-1, ::-1, ::-1]
    w_back = jnp.transpose(back, (3, 5, 2, 4, 0, 1)).reshape(9 * OWN, 3 * ALL)

    xt, conv_int, rim_low, rim_high = forward_conv(features, w_forward)
    up, down = ring("gz", 1), ring("gz", -1)
    from_low = lax.ppermute(rim_high, "gz", up)
    from_high = lax.ppermute(rim_low, "gz", down)

    planes = analyse(features, ex2, ey2)
    planes = lax.all_to_all(planes.reshape(groups, 8, 2 * ALL), "gz", 0, 0, tiled=True)
    table_gz = table_z.reshape(16, groups, plane_count)
    spectrum = jnp.einsum(
        "jgz,gmzc->cjm", table_gz, planes.reshape(groups, 8, plane_count, ALL), precision=highest
    )
    weights32 = spectral_weight.astype(f32)
    mixed = jnp.sum(weights32 * spectrum[:, None], axis=0)
    slab = to_slabs(mixed, table_z)
    layer_out, gt, grad_planes = middle(conv_int, from_low, from_high, slab, grad_out, tables)

    g_low = lax.ppermute(gt[1], "gz", up)
    g_high = lax.ppermute(gt[0], "gz", down)
    g1 = swap(gt, 1)
    g2 = swap(gt, 2)
    g3 = swap(g2, 1)

    grad_planes = lax.all_to_all(grad_planes.reshape(groups, 8, 2 * OWN), "gz", 0, 0, tiled=True)
    grad_modes = jnp.einsum(
        "jgz,gmzc->cjm", table_gz, grad_planes.reshape(groups, 8, plane_count, OWN), precision=highest
    )
    grad_spectral = spectrum[:, None] * grad_modes[None]
    back_terms = jnp.sum(weights32 * grad_modes[None], axis=1)

    local_grad = sum_over_slabs(kernel_grad(xt, gt, g_low, g_high))
    back_int, back_low, back_high = back_conv((gt, g1, g2, g3), w_back)
    back_from_low = lax.ppermute(back_high, "gz", up)
    back_from_high = lax.ppermute(back_low, "gz", down)

    back_modes = lax.dynamic_slice_in_dim(back_terms, first, OWN, 0)
    for bits in range(1, 4):
        there = jnp.bitwise_xor(lax.axis_index("col"), bits) * OWN
        back_modes = back_modes + swap(lax.dynamic_slice_in_dim(back_terms, there, OWN, 0), bits)
    grad_input = last(back_int, back_from_low, back_from_high, to_slabs(back_modes, table_z), tables)

    scaling = 1.0 / math.sqrt(SIDE * SIDE * plane_count * groups)
    grad_conv = jnp.transpose(local_grad.reshape(3, ALL, 3, 3, OWN), (4, 1, 2, 0, 3)).reshape(OWN, ALL, 27) * scaling
    return (layer_out, grad_input, grad_conv, grad_spectral)


def solution(mesh):
    return jax.shard_map(
        local,
        mesh=mesh,
        in_specs=(
            P(None, "gz", None, None),
            P("col", "gz", None, None),
            P("col", None, None),
            P(None, "col", None, "gz"),
        ),
        out_specs=(
            P("col", "gz", None, None),
            P("col", "gz", None, None),
            P("col", None, None),
            P(None, "col", None, "gz"),
        ),
        check_vma=False,
    )
```

time: 888 us -> 203 us (0.23); the launches traced: 872 us -> 202 us
  matrix products: 354 us -> 1.49 us
  local copies, waits for them, and re-layouts: 247 us -> 16.1 us
  other arithmetic: 109 us -> 6.49 us
  blocking collectives: 105 us -> 16 us
  Pallas kernels: 0 us -> 60.5 us
  starting transfers between devices: 9.52 us -> 67.2 us
  between operations: 16.2 us -> 1.07 us
    transpose x1 -> x0, matrix products: 234 us -> none  [local(): jnp.transpose(local_grad, (1, 0, 2, 3, 4))]
    broadcast_in_dim x4 -> x0, local copies, waits for them, and re-layouts: 109 us -> none  [the longest x1 70.9 us: local(): padded[:, None]]
    conv_general_dilated x2 -> x0, matrix products: 101 us -> none  [correlate(): lax.conv_general_dilated(padded[None], kernel, (1, 1, 1), 'VALID', dimens...]
    broadcast_in_dim x3 -> x0, other arithmetic: 92.5 us -> none  [the longest x2 50.1 us: correlate(): padded[None]]
    conv_general_dilated x8 -> x0, local copies, waits for them, and re-layouts: 90.7 us -> none  [correlate(): lax.conv_general_dilated(padded[None], kernel, (1, 1, 1), 'VALID', dimens...]
    all_to_all x6 -> x1, blocking collectives: 105 us -> 16 us  [to_slabs(): lax.all_to_all(columns, 'gz', split_axis=1, concat_axis=2, tiled=True)]
    pallas_call x0 -> x6, Pallas kernels: none -> 60.5 us  [the longest x1 16.2 us: forward_conv(): pl.pallas_call(forward_conv_kernel, out_shape=(jax.ShapeDtypeStruct((2, S...]
    reduce_scatter x1 -> x0, waiting for transfers between devices: 31.4 us -> none  [local(): lax.psum_scatter(contributions, 'col', scatter_dimension=0, tiled=True)]
  transfers between devices with their start and end apart: 6 -> 25, of which waited for: 1 -> 5; matrix products, arithmetic and copies ran while one was open for 57% -> 10% of each run, Pallas kernels for 0% -> 19%
where the time goes in v1:
time: 203 us; the launch traced here: 202 us
  starting transfers between devices  67.2 us (33%)
  Pallas kernels  60.5 us (30%)
  waiting for transfers between devices  33.2 us (16%)
  local copies, waits for them, and re-layouts  16.1 us (8%)
  blocking collectives  16 us (8%)
  other arithmetic  6.49 us (3%)
    ppermute x9, starting transfers between devices, swap(): return lax.ppermute(value, 'col', [(i, i ^ bits) for i in range(count)])  21.3 us
    ppermute x9, waiting for transfers between devices, swap(): return lax.ppermute(value, 'col', [(i, i ^ bits) for i in range(count)])  18.2 us
    pallas_call x1, Pallas kernels, forward_conv(): pl.pallas_call(forward_conv_kernel, out_shape=(jax.ShapeDtypeStruct((2, S...  16.2 us
    all_to_all x1, blocking collectives, to_slabs(): lax.all_to_all(columns, 'gz', split_axis=1, concat_axis=2, tiled=True)  16 us
    all_to_all x1, starting transfers between devices, local(): lax.all_to_all(grad_planes.reshape(groups, 8, 2 * OWN), 'gz', 0, 0, tiled...  14.1 us
    pallas_call x1, Pallas kernels, back_conv(): pl.pallas_call(back_conv_kernel, out_shape=(jax.ShapeDtypeStruct((OWN * 2...  11.8 us
    pallas_call x1, Pallas kernels, middle(): pl.pallas_call(middle_kernel, out_shape=(jax.ShapeDtypeStruct((OWN, 2, SI...  11.1 us
    pallas_call x1, Pallas kernels, kernel_grad(): pl.pallas_call(kernel_grad_kernel, out_shape=jax.ShapeDtypeStruct((3 * AL...  10.8 us
  transfers between devices with their start and end apart: 25, of which 5 were waited for; matrix products, arithmetic and copies ran while one was open for 10% of the time, Pallas kernels for 19%

profile of v1, /device:TPU:1, one launch (start us, length us, event | category | flops | bytes accessed | tf_op | source)
XLA Modules:
  0.0 202.1 jit_solution(13614198594458451953)
XLA Ops:
  0.8 0.6 pad_maximum_fusion.3.ey2_ref
  2.0 5.2 %analyse.1 = f32[256,128]{1,0:T(8,128)} custom-call(bf16[64,2,128,128]{3,2,1,0:T(8,128)(2,1)} %f_ref.3, bf16[32,128]{1,0:T(8,128)(2,1)} %pad_maximum_fusion.2.ex2_ref, bf16[16,256]{1,0:T(8,128)(2,1)} %pad_maximum_fusion.3.ey2_ref), custom_call_target="tpu_custom_call" | custom-call | tf_op jit(solution)/shard_map/analyse/pallas_call | solution.py:160
  7.2 9.7 %all-to-all-start = ((f32[32,8,128]{2,1,0:T(8,128)}), f32[32,8,128]{2,1,0:T(8,128)S(1)}, u32[]{:S(2)}, u32[]{:S(2)}) async-start(f32[32,8,128]{2,1,0:T(8,128)} %bitcast.68), calls=%async_computation | async-start | bytes 262144 | tf_op jit(solution)/shard_map/all_to_all | solution.py:356
  17.0 0.8 reshape.107.w_ref
  17.8 16.2 %forward_conv.1 = (bf16[2,128,64,128]{3,2,1,0:T(8,128)(2,1)}, f32[4096,128]{1,0:T(8,128)}, bf16[16,128,128]{2,1,0:T(8,128)(2,1)}, bf16[16,128,128]{2,1,0:T(8,128)(2,1)}) custom-call(bf16[64,2,128,128]{3,2,1,0:T(8,128)(2,1)} %f_ref.3, bf16[144,192]{1,0:T(8,128)(2,1)} %reshape.107.w_ref), custom_call_target="tpu_custom_call" | custom-call | tf_op jit(solution)/shard_map/forward_conv/pallas_call | solution.py:101
  34.0 1.3 collective-permute-start
  35.3 4.5 %collective-permute-start.1 = (bf16[16,128,128]{2,1,0:T(8,128)(2,1)}, bf16[16,128,128]{2,1,0:T(8,128)(2,1)S(1)}, u32[]{:S(2)}, u32[]{:S(2)}) collective-permute-start(bf16[16,128,128]{2,1,0:T(8,128)(2,1)} %get-tuple-element.16), channel_id=1, source_target_pairs={{0,124},{4,0},{8,4},{12,8},{16,12},{20,16},{24,20},{28,24},{32,28}... | collective-permute-start | bytes 1572872 | tf_op jit(solution)/shard_map/ppermute | solution.py:353
  41.5 0.8 reshape.119
  42.3 3.9 %all-to-all-start.1 = ((f32[32,1,256]{2,1,0:T(1,128)}), f32[32,1,256]{2,1,0:T(1,128)S(1)}, u32[]{:S(2)}, u32[]{:S(2)}) async-start(f32[32,1,256]{2,1,0:T(1,128)} %reshape.119), calls=%async_computation.1 | async-start | bytes 65536 | tf_op jit(solution)/shard_map/all_to_all | solution.py:307
  46.1 0.7 copy.47.ext3_ref
  46.9 6.5 %all-to-all-done.1 = f32[32,1,256]{2,1,0:T(1,128)S(1)} async-done(((f32[32,1,256]{2,1,0:T(1,128)}), f32[32,1,256]{2,1,0:T(1,128)S(1)}, u32[]{:S(2)}, u32[]{:S(2)}) %all-to-all-start.1) | async-done | bytes 32800 | tf_op jit(solution)/shard_map/all_to_all | solution.py:307
  53.8 0.7 reduce
  55.2 0.8 reshape.110.s_ref
  56.0 0.8 copy-done.4
  57.0 11.1 %middle.1 = (bf16[16,2,128,128]{3,2,1,0:T(8,128)(2,1)}, bf16[2,128,16,128]{3,2,1,0:T(8,128)(2,1)}, f32[256,32]{1,0:T(8,128)}) custom-call(f32[4096,128]{1,0:T(8,128)} %get-tuple-element.14.int_ref, bf16[16,128,128]{2,1,0:T(8,128)(2,1)} %copy-done.4, bf16[16,128,128]{2,1,0:T(8,128)(2,1)} %copy-done.6, f32[512,16]{1,0:T(8,128)} %reshape.110.s_ref, ...), custom_call_target="tpu_custom_call" | custom-call | tf_op jit(solution)/shard_map/middle/pallas_call | solution.py:221
  68.1 2.6 %collective-permute-start.3 = (bf16[2,128,16,128]{3,2,1,0:T(8,128)(2,1)}, bf16[2,128,16,128]{3,2,1,0:T(8,128)(2,1)S(1)}, u32[]{:S(2)}, u32[]{:S(2)}) collective-permute-start(bf16[2,128,16,128]{3,2,1,0:T(8,128)(2,1)} %get-tuple-element.18.g0.gt_ref), channel_id=1, source_target_pairs={{0,2},{1,3},{2,0},{3,1},{4,6},{5,7},{6,4},{7,5},{8,10},{9,11},{10,... | collective-permute-start | bytes 3145736 | tf_op jit(solution)/shard_map/ppermute | solution.py:302
  70.9 3.3 %collective-permute-start.5 = (bf16[16,16,27]{1,0,2:T(8,128)(2,1)S(1)}, bf16[16,16,27]{1,0,2:T(8,128)(2,1)S(1)}, u32[]{:S(2)}, u32[]{:S(2)}) collective-permute-start(bf16[16,16,27]{1,0,2:T(8,128)(2,1)S(1)} %get-tuple-element.29), channel_id=1, source_target_pairs={{0,1},{1,0},{2,3},{3,2},{4,5},{5,4},{6,7},{7,6},{8,9},{9,8},{10,11... | collective-permute-start | bytes 41480 | tf_op jit(solution)/shard_map/ppermute | solution.py:302
  74.5 2.6 %collective-permute-start.6 = (bf16[16,16,27]{1,0,2:T(8,128)(2,1)S(1)}, bf16[16,16,27]{1,0,2:T(8,128)(2,1)S(1)}, u32[]{:S(2)}, u32[]{:S(2)}) collective-permute-start(bf16[16,16,27]{1,0,2:T(8,128)(2,1)S(1)} %get-tuple-element.31), channel_id=1, source_target_pairs={{0,2},{1,3},{2,0},{3,1},{4,6},{5,7},{6,4},{7,5},{8,10},{9,11},{10,... | collective-permute-start | bytes 41480 | tf_op jit(solution)/shard_map/ppermute | solution.py:302
  77.1 2.4 %slice_bitcast_fusion = (bf16[128,16,128]{2,1,0:T(8,128)(2,1)}, bf16[128,16,128]{2,1,0:T(8,128)(2,1)}) fusion(bf16[2,128,16,128]{3,2,1,0:T(8,128)(2,1)} %get-tuple-element.18.g0.gt_ref), kind=kLoop, calls=%fused_computation.8 | loop fusion | bytes 2097152 | tf_op jit(solution)/shard_map/squeeze | solution.py:367
  79.6 2.1 %collective-permute-start.14 = (bf16[128,16,128]{2,1,0:T(8,128)(2,1)}, bf16[128,16,128]{2,1,0:T(8,128)(2,1)S(1)}, u32[]{:S(2)}, u32[]{:S(2)}) collective-permute-start(bf16[128,16,128]{2,1,0:T(8,128)(2,1)} %get-tuple-element.24), channel_id=1, source_target_pairs={{0,124},{4,0},{8,4},{12,8},{16,12},{20,16},{24,20},{28,24},{32,28}... | collective-permute-start | bytes 1572872 | tf_op jit(solution)/shard_map/ppermute | solution.py:367
  81.7 17.0 %collective-permute-done.7 = bf16[16,16,27]{1,0,2:T(8,128)(2,1)S(1)} collective-permute-done((bf16[16,16,27]{1,0,2:T(8,128)(2,1)S(1)}, bf16[16,16,27]{1,0,2:T(8,128)(2,1)S(1)}, u32[]{:S(2)}, u32[]{:S(2)}) %collective-permute-start.7) | collective-permute-done | bytes 13856 | tf_op jit(solution)/shard_map/ppermute | solution.py:302
  98.8 1.6 collective-permute-start.2
  100.4 1.6 reshape.121
  102.0 14.1 %all-to-all-start.2 = ((f32[32,1,256]{2,1,0:T(1,128)}), f32[32,1,256]{2,1,0:T(1,128)S(1)}, u32[]{:S(2)}, u32[]{:S(2)}) async-start(f32[32,1,256]{2,1,0:T(1,128)} %reshape.121), calls=%async_computation.2 | async-start | bytes 65536 | tf_op jit(solution)/shard_map/all_to_all | solution.py:372
  116.8 0.9 reshape.111.w_ref
  117.7 5.6 %all-to-all-done.2 = f32[32,1,256]{2,1,0:T(1,128)S(1)} async-done(((f32[32,1,256]{2,1,0:T(1,128)}), f32[32,1,256]{2,1,0:T(1,128)S(1)}, u32[]{:S(2)}, u32[]{:S(2)}) %all-to-all-start.2) | async-done | bytes 32800 | tf_op jit(solution)/shard_map/all_to_all | solution.py:372
  123.3 0.7 reduce.1
  124.7 1.3 broadcast_multiply_fusion
  126.0 0.9 copy-done.3
  126.9 10.8 %kernel_grad.1 = f32[192,144]{1,0:T(8,128)} custom-call(bf16[2,128,64,128]{3,2,1,0:T(8,128)(2,1)} %get-tuple-element.23.xt_ref, bf16[2,128,16,128]{3,2,1,0:T(8,128)(2,1)} %get-tuple-element.18.g0.gt_ref, bf16[128,16,128]{2,1,0:T(8,128)(2,1)} %collective-permute-done.13.gl_ref, bf16[128,16,128]{2,1,0:T(8,128)(2,1)} %copy-done.3), custom_call_target="tpu_custom_call" | custom-call | tf_op jit(solution)/shard_map/kernel_grad/pallas_call | solution.py:264
  137.7 1.0 collective-permute-start.17
  138.7 1.1 collective-permute-start.16
  139.9 3.0 %collective-permute-done.17 = f32[192,144]{1,0:T(8,128)S(1)} collective-permute-done((f32[192,144]{1,0:T(8,128)}, f32[192,144]{1,0:T(8,128)S(1)}, u32[]{:S(2)}, u32[]{:S(2)}) %collective-permute-start.17) | collective-permute-done | bytes 110624 | tf_op jit(solution)/shard_map/ppermute | solution.py:320
  142.9 4.2 %collective-permute-start.10 = (f32[16,16,8]{0,2,1:T(8,128)S(1)}, f32[16,16,8]{0,2,1:T(8,128)S(1)}, u32[]{:S(2)}, u32[]{:S(2)}) collective-permute-start(f32[16,16,8]{0,2,1:T(8,128)S(1)} %get-tuple-element.32), channel_id=1, source_target_pairs={{0,1},{1,0},{2,3},{3,2},{4,5},{5,4},{6,7},{7,6},{8,9},{9,8},{10,11... | collective-permute-start | bytes 24584 | tf_op jit(solution)/shard_map/ppermute | solution.py:302
  147.1 5.2 %collective-permute-start.12 = (f32[16,16,8]{0,2,1:T(8,128)S(1)}, f32[16,16,8]{0,2,1:T(8,128)S(1)}, u32[]{:S(2)}, u32[]{:S(2)}) collective-permute-start(f32[16,16,8]{0,2,1:T(8,128)S(1)} %get-tuple-element.33), channel_id=1, source_target_pairs={{0,3},{1,2},{2,1},{3,0},{4,7},{5,6},{6,5},{7,4},{8,11},{9,10},{10,... | collective-permute-start | bytes 24584 | tf_op jit(solution)/shard_map/ppermute | solution.py:302
  152.3 1.2 collective-permute-start.11
  153.5 1.0 add_add_fusion.1
  154.5 1.0 collective-permute-start.20
  155.4 1.2 collective-permute-start.19
  156.7 1.2 collective-permute-done.11
  158.3 11.8 %back_conv.1 = (f32[4096,128]{1,0:T(8,128)}, bf16[16,128,128]{2,1,0:T(8,128)(2,1)}, bf16[16,128,128]{2,1,0:T(8,128)(2,1)}) custom-call(bf16[2,128,16,128]{3,2,1,0:T(8,128)(2,1)} %get-tuple-element.18.g0.gt_ref, bf16[2,128,16,128]{3,2,1,0:T(8,128)(2,1)} %collective-permute-done.2.g1, bf16[2,128,16,128]{3,2,1,0:T(8,128)(2,1)} %copy-done.2, ...), custom_call_target="tpu_custom_call" | custom-call | tf_op jit(solution)/shard_map/back_conv/pallas_call | solution.py:126
  170.1 5.7 %collective-permute-start.9 = (bf16[16,128,128]{2,1,0:T(8,128)(2,1)}, bf16[16,128,128]{2,1,0:T(8,128)(2,1)S(1)}, u32[]{:S(2)}, u32[]{:S(2)}) collective-permute-start(bf16[16,128,128]{2,1,0:T(8,128)(2,1)} %get-tuple-element.21), channel_id=1, source_target_pairs={{0,124},{4,0},{8,4},{12,8},{16,12},{20,16},{24,20},{28,24},{32,28}... | collective-permute-start | bytes 1572872 | tf_op jit(solution)/shard_map/ppermute | solution.py:382
  176.5 16.0 %all_to_all.40 = f32[32,1,256]{2,1,0:T(1,128)S(1)} all-to-all(f32[32,1,256]{2,1,0:T(1,128)S(1)} %reshape.123), channel_id=1, replica_groups=mesh['gz'=32,'col'=4] {'gz'}, dimensions={0} | all-to-all | bytes 65536 | tf_op jit(solution)/shard_map/all_to_all | solution.py:307
  192.5 0.7 reduce.2
  193.9 0.8 reshape.114.s_ref
  195.0 0.7 copy.56
  195.7 0.8 copy-done.5
  196.7 5.4 %last.1 = bf16[16,2,128,128]{3,2,1,0:T(8,128)(2,1)} custom-call(f32[4096,128]{1,0:T(8,128)} %get-tuple-element.19.int_ref, bf16[16,128,128]{2,1,0:T(8,128)(2,1)} %copy-done.5, bf16[16,128,128]{2,1,0:T(8,128)(2,1)} %copy-done.7, f32[512,16]{1,0:T(8,128)} %reshape.114.s_ref, bf16[128,48]{1,0:T(8,128)(2,1)} %copy.47.ext3_ref, bf16[16,128]{1,0:T(8,128)(2,1)} %copy-done.8, ...), custom_call_target="tpu_custom_call" | custom-call | tf_op jit(solution)/shard_map/last/pallas_call | solution.py:287
  (81 shorter events, 8.3 us)
Async XLA Ops:
  0.6 16.3 %copy-start = (bf16[16,64,27]{1,0,2:T(8,128)(2,1)S(1)}, bf16[16,64,27]{1,0,2:T(8,128)(2,1)}, u32[]{:S(2)}) copy-start(bf16[16,64,27]{1,0,2:T(8,128)(2,1)} %param.6) | copy-start | bytes 165892
  0.8 33.2 %copy-start.8 = (bf16[16,128]{1,0:T(8,128)(2,1)}, bf16[16,128]{1,0:T(8,128)(2,1)S(1)}, u32[]{:S(2)}) copy-start(bf16[16,128]{1,0:T(8,128)(2,1)S(1)} %get-tuple-element.37.eyh_ref) | copy-start | bytes 12292
  0.8 33.2 %copy-start.9 = (bf16[16,128]{1,0:T(8,128)(2,1)}, bf16[16,128]{1,0:T(8,128)(2,1)S(1)}, u32[]{:S(2)}) copy-start(bf16[16,128]{1,0:T(8,128)(2,1)S(1)} %get-tuple-element.38.eyl_ref) | copy-start | bytes 12292
  2.0 38.6 %copy-start.1 = (bf16[64,16,16,8]{0,3,2,1:T(8,128)(2,1)S(1)}, bf16[64,16,16,8]{0,3,2,1:T(8,128)(2,1)}, u32[]{:S(2)}) copy-start(bf16[64,16,16,8]{0,3,2,1:T(8,128)(2,1)} %param.7) | copy-start | bytes 786436
  7.2 32.7 %all-to-all-start = ((f32[32,8,128]{2,1,0:T(8,128)}), f32[32,8,128]{2,1,0:T(8,128)S(1)}, u32[]{:S(2)}, u32[]{:S(2)}) async-start(f32[32,8,128]{2,1,0:T(8,128)} %bitcast.68), calls=%async_computation | async-start | bytes 262144 | tf_op jit(solution)/shard_map/all_to_all | solution.py:356
  34.0 22.0 %collective-permute-start = (bf16[16,128,128]{2,1,0:T(8,128)(2,1)}, bf16[16,128,128]{2,1,0:T(8,128)(2,1)S(1)}, u32[]{:S(2)}, u32[]{:S(2)}) collective-permute-start(bf16[16,128,128]{2,1,0:T(8,128)(2,1)} %get-tuple-element.15), channel_id=1, source_target_pairs={{0,4},{4,8},{8,12},{12,16},{16,20},{20,24},{24,28},{28,32},{32,36}... | collective-permute-start | bytes 1572872 | tf_op jit(solution)/shard_map/ppermute | solution.py:352
  35.3 20.8 %collective-permute-start.1 = (bf16[16,128,128]{2,1,0:T(8,128)(2,1)}, bf16[16,128,128]{2,1,0:T(8,128)(2,1)S(1)}, u32[]{:S(2)}, u32[]{:S(2)}) collective-permute-start(bf16[16,128,128]{2,1,0:T(8,128)(2,1)} %get-tuple-element.16), channel_id=1, source_target_pairs={{0,124},{4,0},{8,4},{12,8},{16,12},{20,16},{24,20},{28,24},{32,28}... | collective-permute-start | bytes 1572872 | tf_op jit(solution)/shard_map/ppermute | solution.py:353
  42.3 11.0 %all-to-all-start.1 = ((f32[32,1,256]{2,1,0:T(1,128)}), f32[32,1,256]{2,1,0:T(1,128)S(1)}, u32[]{:S(2)}, u32[]{:S(2)}) async-start(f32[32,1,256]{2,1,0:T(1,128)} %reshape.119), calls=%async_computation.1 | async-start | bytes 65536 | tf_op jit(solution)/shard_map/all_to_all | solution.py:307
  56.0 0.8 copy-start.4
  56.0 1.0 copy-start.6
  68.1 48.0 %collective-permute-start.3 = (bf16[2,128,16,128]{3,2,1,0:T(8,128)(2,1)}, bf16[2,128,16,128]{3,2,1,0:T(8,128)(2,1)S(1)}, u32[]{:S(2)}, u32[]{:S(2)}) collective-permute-start(bf16[2,128,16,128]{3,2,1,0:T(8,128)(2,1)} %get-tuple-element.18.g0.gt_ref), channel_id=1, source_target_pairs={{0,2},{1,3},{2,0},{3,1},{4,6},{5,7},{6,4},{7,5},{8,10},{9,11},{10,... | collective-permute-start | bytes 3145736 | tf_op jit(solution)/shard_map/ppermute | solution.py:302
  70.9 10.8 %collective-permute-start.5 = (bf16[16,16,27]{1,0,2:T(8,128)(2,1)S(1)}, bf16[16,16,27]{1,0,2:T(8,128)(2,1)S(1)}, u32[]{:S(2)}, u32[]{:S(2)}) collective-permute-start(bf16[16,16,27]{1,0,2:T(8,128)(2,1)S(1)} %get-tuple-element.29), channel_id=1, source_target_pairs={{0,1},{1,0},{2,3},{3,2},{4,5},{5,4},{6,7},{7,6},{8,9},{9,8},{10,11... | collective-permute-start | bytes 41480 | tf_op jit(solution)/shard_map/ppermute | solution.py:302
  74.2 24.5 %collective-permute-start.7 = (bf16[16,16,27]{1,0,2:T(8,128)(2,1)S(1)}, bf16[16,16,27]{1,0,2:T(8,128)(2,1)S(1)}, u32[]{:S(2)}, u32[]{:S(2)}) collective-permute-start(bf16[16,16,27]{1,0,2:T(8,128)(2,1)S(1)} %get-tuple-element.30), channel_id=1, source_target_pairs={{0,3},{1,2},{2,1},{3,0},{4,7},{5,6},{6,5},{7,4},{8,11},{9,10},{10,... | collective-permute-start | bytes 41480 | tf_op jit(solution)/shard_map/ppermute | solution.py:302
  74.5 24.2 %collective-permute-start.6 = (bf16[16,16,27]{1,0,2:T(8,128)(2,1)S(1)}, bf16[16,16,27]{1,0,2:T(8,128)(2,1)S(1)}, u32[]{:S(2)}, u32[]{:S(2)}) collective-permute-start(bf16[16,16,27]{1,0,2:T(8,128)(2,1)S(1)} %get-tuple-element.31), channel_id=1, source_target_pairs={{0,2},{1,3},{2,0},{3,1},{4,6},{5,7},{6,4},{7,5},{8,10},{9,11},{10,... | collective-permute-start | bytes 41480 | tf_op jit(solution)/shard_map/ppermute | solution.py:302
  79.6 46.4 %collective-permute-start.14 = (bf16[128,16,128]{2,1,0:T(8,128)(2,1)}, bf16[128,16,128]{2,1,0:T(8,128)(2,1)S(1)}, u32[]{:S(2)}, u32[]{:S(2)}) collective-permute-start(bf16[128,16,128]{2,1,0:T(8,128)(2,1)} %get-tuple-element.24), channel_id=1, source_target_pairs={{0,124},{4,0},{8,4},{12,8},{16,12},{20,16},{24,20},{28,24},{32,28}... | collective-permute-start | bytes 1572872 | tf_op jit(solution)/shard_map/ppermute | solution.py:367
  81.7 44.3 %collective-permute-start.13 = (bf16[128,16,128]{2,1,0:T(8,128)(2,1)}, bf16[128,16,128]{2,1,0:T(8,128)(2,1)}, u32[]{:S(2)}, u32[]{:S(2)}) collective-permute-start(bf16[128,16,128]{2,1,0:T(8,128)(2,1)} %get-tuple-element.25), channel_id=1, source_target_pairs={{0,4},{4,8},{8,12},{12,16},{16,20},{20,24},{24,28},{28,32},{32,36}... | collective-permute-start | bytes 1572872 | tf_op jit(solution)/shard_map/ppermute | solution.py:366
  98.8 59.4 %collective-permute-start.2 = (bf16[2,128,16,128]{3,2,1,0:T(8,128)(2,1)}, bf16[2,128,16,128]{3,2,1,0:T(8,128)(2,1)}, u32[]{:S(2)}, u32[]{:S(2)}) collective-permute-start(bf16[2,128,16,128]{3,2,1,0:T(8,128)(2,1)} %get-tuple-element.18.g0.gt_ref), channel_id=1, source_target_pairs={{0,1},{1,0},{2,3},{3,2},{4,5},{5,4},{6,7},{7,6},{8,9},{9,8},{10,11... | collective-permute-start | bytes 3145736 | tf_op jit(solution)/shard_map/ppermute | solution.py:302
  102.0 21.3 %all-to-all-start.2 = ((f32[32,1,256]{2,1,0:T(1,128)}), f32[32,1,256]{2,1,0:T(1,128)S(1)}, u32[]{:S(2)}, u32[]{:S(2)}) async-start(f32[32,1,256]{2,1,0:T(1,128)} %reshape.121), calls=%async_computation.2 | async-start | bytes 65536 | tf_op jit(solution)/shard_map/all_to_all | solution.py:372
  116.1 21.6 %copy-start.2 = (bf16[2,128,16,128]{3,2,1,0:T(8,128)(2,1)}, bf16[2,128,16,128]{3,2,1,0:T(8,128)(2,1)S(1)}, u32[]{:S(2)}) copy-start(bf16[2,128,16,128]{3,2,1,0:T(8,128)(2,1)S(1)} %collective-permute-done.3.g2) | copy-start | bytes 3145732
  116.1 42.1 %collective-permute-start.4 = (bf16[2,128,16,128]{3,2,1,0:T(8,128)(2,1)S(1)}, bf16[2,128,16,128]{3,2,1,0:T(8,128)(2,1)}, u32[]{:S(2)}, u32[]{:S(2)}) collective-permute-start(bf16[2,128,16,128]{3,2,1,0:T(8,128)(2,1)S(1)} %collective-permute-done.3.g2), channel_id=1, source_target_pairs={{0,1},{1,0},{2,3},{3,2},{4,5},{5,4},{6,7},{7,6},{8,9},{9,8},{10,11... | collective-permute-start | bytes 3145736 | tf_op jit(solution)/shard_map/ppermute | solution.py:302
  126.0 0.9 copy-start.3
  137.7 5.2 %collective-permute-start.17 = (f32[192,144]{1,0:T(8,128)}, f32[192,144]{1,0:T(8,128)S(1)}, u32[]{:S(2)}, u32[]{:S(2)}) collective-permute-start(f32[192,144]{1,0:T(8,128)} %kernel_grad.1), channel_id=1, source_target_pairs={{0,12},{4,0},{8,4},{12,8},{16,28},{20,16},{24,20},{28,24},{32,44},... | collective-permute-start | bytes 331784 | tf_op jit(solution)/shard_map/ppermute | solution.py:320
  138.7 8.4 %collective-permute-start.16 = (f32[192,144]{1,0:T(8,128)}, f32[192,144]{1,0:T(8,128)S(1)}, u32[]{:S(2)}, u32[]{:S(2)}) collective-permute-start(f32[192,144]{1,0:T(8,128)} %kernel_grad.1), channel_id=1, source_target_pairs={{0,8},{4,12},{8,0},{12,4},{16,24},{20,28},{24,16},{28,20},{32,40},... | collective-permute-start | bytes 331784 | tf_op jit(solution)/shard_map/ppermute | solution.py:320
  139.8 12.5 %collective-permute-start.15 = (f32[192,144]{1,0:T(8,128)}, f32[192,144]{1,0:T(8,128)S(1)}, u32[]{:S(2)}, u32[]{:S(2)}) collective-permute-start(f32[192,144]{1,0:T(8,128)} %kernel_grad.1), channel_id=1, source_target_pairs={{0,4},{4,8},{8,12},{12,0},{16,20},{20,24},{24,28},{28,16},{32,36},... | collective-permute-start | bytes 331784 | tf_op jit(solution)/shard_map/ppermute | solution.py:320
  142.9 11.6 %collective-permute-start.10 = (f32[16,16,8]{0,2,1:T(8,128)S(1)}, f32[16,16,8]{0,2,1:T(8,128)S(1)}, u32[]{:S(2)}, u32[]{:S(2)}) collective-permute-start(f32[16,16,8]{0,2,1:T(8,128)S(1)} %get-tuple-element.32), channel_id=1, source_target_pairs={{0,1},{1,0},{2,3},{3,2},{4,5},{5,4},{6,7},{7,6},{8,9},{9,8},{10,11... | collective-permute-start | bytes 24584 | tf_op jit(solution)/shard_map/ppermute | solution.py:302
  147.1 8.3 %collective-permute-start.12 = (f32[16,16,8]{0,2,1:T(8,128)S(1)}, f32[16,16,8]{0,2,1:T(8,128)S(1)}, u32[]{:S(2)}, u32[]{:S(2)}) collective-permute-start(f32[16,16,8]{0,2,1:T(8,128)S(1)} %get-tuple-element.33), channel_id=1, source_target_pairs={{0,3},{1,2},{2,1},{3,0},{4,7},{5,6},{6,5},{7,4},{8,11},{9,10},{10,... | collective-permute-start | bytes 24584 | tf_op jit(solution)/shard_map/ppermute | solution.py:302
  152.3 5.6 %collective-permute-start.11 = (f32[16,16,8]{0,2,1:T(8,128)S(1)}, f32[16,16,8]{0,2,1:T(8,128)S(1)}, u32[]{:S(2)}, u32[]{:S(2)}) collective-permute-start(f32[16,16,8]{0,2,1:T(8,128)S(1)} %get-tuple-element.34), channel_id=1, source_target_pairs={{0,2},{1,3},{2,0},{3,1},{4,6},{5,7},{6,4},{7,5},{8,10},{9,11},{10,... | collective-permute-start | bytes 24584 | tf_op jit(solution)/shard_map/ppermute | solution.py:302
  154.5 21.3 %collective-permute-start.20 = (f32[192,144]{1,0:T(8,128)S(1)}, f32[192,144]{1,0:T(8,128)S(1)}, u32[]{:S(2)}, u32[]{:S(2)}) collective-permute-start(f32[192,144]{1,0:T(8,128)S(1)} %add_add_fusion.1), channel_id=1, source_target_pairs={{0,48},{4,52},{8,56},{12,60},{16,0},{20,4},{24,8},{28,12},{32,16},... | collective-permute-start | bytes 331784 | tf_op jit(solution)/shard_map/ppermute | solution.py:320
  155.4 20.3 %collective-permute-start.19 = (f32[192,144]{1,0:T(8,128)S(1)}, f32[192,144]{1,0:T(8,128)S(1)}, u32[]{:S(2)}, u32[]{:S(2)}) collective-permute-start(f32[192,144]{1,0:T(8,128)S(1)} %add_add_fusion.1), channel_id=1, source_target_pairs={{0,32},{4,36},{8,40},{12,44},{16,48},{20,52},{24,56},{28,60},{32,0... | collective-permute-start | bytes 331784 | tf_op jit(solution)/shard_map/ppermute | solution.py:320
  157.8 17.9 %collective-permute-start.18 = (f32[192,144]{1,0:T(8,128)S(1)}, f32[192,144]{1,0:T(8,128)S(1)}, u32[]{:S(2)}, u32[]{:S(2)}) collective-permute-start(f32[192,144]{1,0:T(8,128)S(1)} %add_add_fusion.1), channel_id=1, source_target_pairs={{0,16},{4,20},{8,24},{12,28},{16,32},{20,36},{24,40},{28,44},{32,4... | collective-permute-start | bytes 331784 | tf_op jit(solution)/shard_map/ppermute | solution.py:320
  170.0 25.7 %collective-permute-start.8 = (bf16[16,128,128]{2,1,0:T(8,128)(2,1)}, bf16[16,128,128]{2,1,0:T(8,128)(2,1)S(1)}, u32[]{:S(2)}, u32[]{:S(2)}) collective-permute-start(bf16[16,128,128]{2,1,0:T(8,128)(2,1)} %get-tuple-element.20), channel_id=1, source_target_pairs={{0,4},{4,8},{8,12},{12,16},{16,20},{20,24},{24,28},{28,32},{32,36}... | collective-permute-start | bytes 1572872 | tf_op jit(solution)/shard_map/ppermute | solution.py:381
  170.1 25.7 %collective-permute-start.9 = (bf16[16,128,128]{2,1,0:T(8,128)(2,1)}, bf16[16,128,128]{2,1,0:T(8,128)(2,1)S(1)}, u32[]{:S(2)}, u32[]{:S(2)}) collective-permute-start(bf16[16,128,128]{2,1,0:T(8,128)(2,1)} %get-tuple-element.21), channel_id=1, source_target_pairs={{0,124},{4,0},{8,4},{12,8},{16,12},{20,16},{24,20},{28,24},{32,28}... | collective-permute-start | bytes 1572872 | tf_op jit(solution)/shard_map/ppermute | solution.py:382
  175.8 18.9 %collective-permute-start.21 = (f32[192,144]{1,0:T(8,128)S(1)}, f32[192,144]{1,0:T(8,128)S(1)}, u32[]{:S(2)}, u32[]{:S(2)}) collective-permute-start(f32[192,144]{1,0:T(8,128)S(1)} %add_add_fusion), channel_id=1, source_target_pairs={{0,64},{4,68},{8,72},{12,76},{16,80},{20,84},{24,88},{28,92},{32,9... | collective-permute-start | bytes 331784 | tf_op jit(solution)/shard_map/ppermute | solution.py:320
  195.7 0.8 copy-start.5
  195.7 1.0 copy-start.7

commit v2 on v0

v2 whole, which is shorter than its diff:
```python
import math

import jax
import jax.numpy as jnp
import numpy as np
from jax import lax
from jax.experimental import pallas as pl
from jax.experimental.pallas import tpu as pltpu
from jax.sharding import PartitionSpec as P

highest = lax.Precision.HIGHEST
f32 = jnp.float32
bf16 = jnp.bfloat16
SIDE = 128
OWN = 16
ALL = 64
STRIP = 16
STRIPS = SIDE // STRIP
CHUNKS = 4
CONV_FLOPS = 2 * 27 * ALL * OWN * 2 * SIDE * SIDE
GELU_A = math.sqrt(2.0 / math.pi)
GELU_B = 0.044715


def basis(length, mode_count):
    indices = np.arange(mode_count)
    middle = mode_count // 2
    frequency = np.where(indices <= middle, indices, indices - middle)
    radians = frequency[:, None] * np.arange(length)[None, :] % length * (2.0 * math.pi / length)
    tables = np.where((indices <= middle)[:, None], np.cos(radians), np.sin(radians))
    return (tables * math.sqrt(2.0 / length)).astype(np.float32)


def host_split(table):
    high = table.astype(bf16)
    return high, (table - high.astype(np.float32)).astype(bf16)


def call(kernel, grid, ins, outs, scratch, *args):
    def spec(entry, shape):
        if entry == "hbm":
            return pl.BlockSpec(memory_space=pl.ANY)
        if entry is None:
            return pl.BlockSpec(shape, lambda k: (0,) * len(shape))
        return pl.BlockSpec(*entry)

    result = pl.pallas_call(
        kernel,
        grid=(grid,),
        in_specs=[spec(entry, value.shape) for entry, value in zip(ins, args)],
        out_specs=tuple(spec(entry, shape) for shape, _, entry in outs),
        out_shape=tuple(jax.ShapeDtypeStruct(shape, dtype) for shape, dtype, _ in outs),
        scratch_shapes=scratch,
        cost_estimate=pl.CostEstimate(flops=CONV_FLOPS, bytes_accessed=8 << 20, transcendentals=0),
        compiler_params=pltpu.CompilerParams(dimension_semantics=("arbitrary",)),
    )(*args)
    return result if len(outs) > 1 else result[0]


def whole(kernel, ins, outs, scratch, *args):
    def spec(kind):
        return pl.BlockSpec(memory_space=pl.ANY) if kind == "hbm" else pl.BlockSpec()

    def held(kind, value):
        space = {"vmem": pltpu.VMEM, "hbm": pltpu.HBM}.get(kind)
        return value if space is None else pltpu.with_memory_space_constraint(value, space)

    result = pl.pallas_call(
        kernel,
        in_specs=[spec(kind) for kind in ins],
        out_specs=tuple(spec(kind) for _, _, kind in outs),
        out_shape=tuple(
            pltpu.VMEM(shape, dtype) if kind == "vmem" else jax.ShapeDtypeStruct(shape, dtype)
            for shape, dtype, kind in outs
        ),
        scratch_shapes=scratch,
        cost_estimate=pl.CostEstimate(flops=CONV_FLOPS, bytes_accessed=8 << 20, transcendentals=0),
        compiler_params=pltpu.CompilerParams(vmem_limit_bytes=24 << 20),
    )(*(held(kind, value) for kind, value in zip(ins, args)))
    return result if len(outs) > 1 else result[0]


def chunk_copy(source, target, sem, k, size):
    rows = pl.ds(k * size, size)
    return pltpu.make_async_copy(source.at[rows], target.at[rows], sem.at[k])


def split2(value):
    high = value.astype(bf16)
    low = (value - high.astype(f32)).astype(bf16)
    return high, low


def dot(a, b):
    return jnp.dot(a, b, preferred_element_type=f32)


def dot_nt(a, b):
    return lax.dot_general(a, b, (((1,), (1,)), ((), ())), preferred_element_type=f32)


def fetch(sources, targets, sems):
    def copy(n, k):
        rows = pl.ds(k * STRIP, STRIP)
        return pltpu.make_async_copy(sources[n].at[:, rows], targets[n].at[:, rows], sems.at[n, k])

    def start(k):
        for n in range(len(sources)):
            copy(n, k).start()

    def wait(k):
        for n in range(len(sources)):
            copy(n, k).wait()

    step = pl.program_id(0)

    @pl.when(step == 0)
    def _():
        for k in (STRIPS - 1, *range(STRIPS - 1)):
            start(k)
        wait(STRIPS - 1)
        wait(0)

    @pl.when(step < STRIPS - 2)
    def _():
        wait(step + 1)


def conv_strip(slab, strip, w_ref, planes, turn_ref, flip):
    rows = 3 * OWN
    needed = []
    for z in range(2):
        offsets = [a for a in range(3) if (z + a - 1 if flip else z - a + 1) in planes]
        needed.append((min(offsets), max(offsets) + 1))
    for u in range(0, STRIP, 2):
        sums = {}
        for z in range(2):
            columns = []
            for v in range(2):
                x = strip * STRIP + u + v
                near = [(x + SIDE - 1) % SIDE, x, (x + 1) % SIDE]
                columns.append(jnp.concatenate([slab(z, n) for n in (near[::-1] if flip else near)], axis=0))
            low, high = needed[z]
            r = dot(w_ref[low * rows : high * rows, :], jnp.concatenate(columns, axis=1))
            for a in range(low, high):
                plane = z + a - 1 if flip else z - a + 1
                term = r[(a - low) * rows : (a - low + 1) * rows]
                sums[plane] = sums[plane] + term if plane in sums else term
        for place, plane in enumerate(planes):
            for v in range(2):
                half = sums[plane][:, v * SIDE : (v + 1) * SIDE]
                c0, c1, c2 = (half[c * OWN : (c + 1) * OWN] for c in range(3))
                if flip:
                    c0, c2 = c2, c0
                total = c1 + pltpu.roll(c0, 1, axis=1) + pltpu.roll(c2, SIDE - 1, axis=1)
                turn_ref[pl.ds(place * OWN * STRIP + u + v, OWN, stride=STRIP), :] = total


def turned(turn_ref, place):
    size = OWN * STRIP
    return turn_ref[place * size : (place + 1) * size, :].reshape(OWN, STRIP, SIDE)


def front_kernel(f_ref, w_ref, xt_ref, int_ref, low_ref, high_ref, field_ref, wide_ref, turn_ref):
    step = pl.program_id(0)

    @pl.when(step < STRIPS)
    def _():
        for z in range(2):
            wide_ref[z] = f_ref[:, z].astype(f32).reshape(ALL * STRIP, SIDE)
        for z in range(2):
            for u in range(STRIP):
                row = wide_ref[z, pl.ds(u, ALL, stride=STRIP), :].astype(bf16)
                field_ref[z, step * STRIP + u] = row
                xt_ref[z, u] = row

    @pl.when(step >= 2)
    def _():
        strip = lax.rem(step - 1, STRIPS)
        conv_strip(lambda z, x: field_ref[z, x], strip, w_ref, (-1, 0, 1, 2), turn_ref, False)
        write_strip(turn_ref, int_ref, low_ref, high_ref)


def write_strip(turn_ref, int_ref, low_ref, high_ref):
    low_ref[...] = turned(turn_ref, 0).astype(bf16)
    for z in range(2):
        int_ref[:, z] = turned(turn_ref, z + 1).astype(bf16)
    high_ref[...] = turned(turn_ref, 3).astype(bf16)


def front(features, w):
    def late(k):
        return lax.select(k < 2, 1, lax.rem(k - 1, STRIPS))

    def early(k):
        return jnp.minimum(k, STRIPS - 1)

    rim = ((OWN, SIDE, SIDE), bf16, ((OWN, STRIP, SIDE), lambda k: (0, late(k), 0)))
    return call(
        front_kernel, STRIPS + 2,
        (((ALL, 2, STRIP, SIDE), lambda k: (0, 0, early(k), 0)), None),
        (
            ((2, SIDE, ALL, SIDE), bf16, ((2, STRIP, ALL, SIDE), lambda k: (0, early(k), 0, 0))),
            ((OWN, 2, SIDE, SIDE), bf16, ((OWN, 2, STRIP, SIDE), lambda k: (0, 0, late(k), 0))),
            rim,
            rim,
        ),
        [
            pltpu.VMEM((2, SIDE, ALL, SIDE), bf16),
            pltpu.VMEM((2, ALL * STRIP, SIDE), f32),
            pltpu.VMEM((4 * OWN * STRIP, SIDE), f32),
        ],
        features, w,
    )


INNER_OUT = ((OWN, 2, SIDE, SIDE), bf16, ((OWN, 2, STRIP, SIDE), lambda k: (0, 0, k, 0)))
RIM_OUT = ((OWN, SIDE, SIDE), bf16, ((OWN, STRIP, SIDE), lambda k: (0, k, 0)))


def back_conv_kernel(g0, g1, g2, g3, w_ref, int_ref, low_ref, high_ref, f0, f1, f2, f3, turn_ref, sems):
    fields = (f0, f1, f2, f3)
    fetch((g0, g1, g2, g3), fields, sems)

    def slab(z, x):
        return jnp.concatenate([f[z, x] for f in fields], axis=0)

    conv_strip(slab, pl.program_id(0), w_ref, (-1, 0, 1, 2), turn_ref, True)
    write_strip(turn_ref, int_ref, low_ref, high_ref)


def back_conv(shares, w):
    return call(
        back_conv_kernel, STRIPS, ("hbm", "hbm", "hbm", "hbm", None),
        (INNER_OUT, RIM_OUT, RIM_OUT),
        [pltpu.VMEM((2, SIDE, OWN, SIDE), bf16)] * 4
        + [pltpu.VMEM((4 * OWN * STRIP, SIDE), f32), pltpu.SemaphoreType.DMA((4, STRIPS))],
        *shares, w,
    )


def finish_modes(g_ref, ey2, out_ref, width):
    for kx in range(16):
        high, low = split2(g_ref[kx * width : (kx + 1) * width, :])
        out_ref[kx * 16 : (kx + 1) * 16, :width] = dot_nt(ey2, jnp.concatenate([high, low], axis=1))


def analyse_kernel(f_hbm, ex2_ref, ey2_ref, out_ref, f_ref, g_ref, sem):
    size = ALL // CHUNKS
    for k in range(CHUNKS):
        chunk_copy(f_hbm, f_ref, sem, k, size).start()

    def chunk(k, carry):
        chunk_copy(f_hbm, f_ref, sem, k, size).wait()
        ex2 = ex2_ref[...]
        for u in range(size):
            ch = k * size + u
            r = dot(ex2, jnp.concatenate([f_ref[ch, 0], f_ref[ch, 1]], axis=1))
            g = r[:16] + r[16:]
            g_ref[pl.ds(ch, 16, stride=2 * ALL), :] = g[:, :SIDE]
            g_ref[pl.ds(ch + ALL, 16, stride=2 * ALL), :] = g[:, SIDE:]
        return carry

    lax.fori_loop(0, CHUNKS, chunk, 0)
    finish_modes(g_ref, ey2_ref[...], out_ref, 2 * ALL)


def analyse(features, ex2, ey2):
    return whole(
        analyse_kernel, ("hbm", None, None), (((256, 2 * ALL), f32, None),),
        [
            pltpu.VMEM((ALL, 2, SIDE, SIDE), bf16),
            pltpu.VMEM((16 * 2 * ALL, SIDE), f32),
            pltpu.SemaphoreType.DMA((CHUNKS,)),
        ],
        features, ex2, ey2,
    )


def along_y(s_ref, eyh_ref, eyl_ref, t_ref):
    sides = [
        jnp.concatenate([s_ref[pl.ds(half * 2 + z, 16, stride=4), :] for half in range(2)], axis=1)
        for z in range(2)
    ]
    high, low = split2(jnp.concatenate(sides, axis=0))
    lane = lax.broadcasted_iota(jnp.int32, (32, 256), 1)
    channel = lane % SIDE // 8
    eyh = eyh_ref[...]
    eyl = eyl_ref[...]
    for o in range(OWN):
        keep = (channel == o).astype(bf16)
        own = high * keep
        t_ref[o * 32 : (o + 1) * 32, :] = dot(own, eyh) + dot(low * keep, eyh) + dot(own, eyl)


def along_x(t_ref, ext3, o):
    t = jnp.concatenate([t_ref[pl.ds(o * 32, 16), :], t_ref[pl.ds(o * 32 + 16, 16), :]], axis=1)
    high, low = split2(t)
    return dot(ext3, jnp.concatenate([high, high, low], axis=0))


def middle_kernel(
    int_hbm, go_hbm, fl_ref, fh_ref, s_ref, ex2_ref, ey2_ref, ext3_ref, eyh_ref, eyl_ref,
    out_hbm, gt_ref, first_ref, last_ref, modes_ref,
    int_ref, go_ref, out_ref, t_ref, g_ref, turn_ref, wide_ref, in_sem, go_sem, out_sem,
):
    size = OWN // CHUNKS
    for k in range(CHUNKS):
        chunk_copy(int_hbm, int_ref, in_sem, k, size).start()
        chunk_copy(go_hbm, go_ref, go_sem, k, size).start()
    along_y(s_ref, eyh_ref, eyl_ref, t_ref)

    def chunk(k, carry):
        chunk_copy(int_hbm, int_ref, in_sem, k, size).wait()
        chunk_copy(go_hbm, go_ref, go_sem, k, size).wait()
        for u in range(size):
            o = k * size + u
            smooth = along_x(t_ref, ext3_ref[...], o)
            halves = []
            for z in range(2):
                rim = (fl_ref if z == 0 else fh_ref)[o].astype(f32)
                p = int_ref[o, z].astype(f32) + rim + smooth[:, z * SIDE : (z + 1) * SIDE]
                square = p * p
                t = jnp.tanh(p * (GELU_A + GELU_A * GELU_B * square))
                half = 0.5 + 0.5 * t
                out_ref[o, z] = (p * half).astype(bf16)
                slope = half + p * (0.5 - 0.5 * (t * t)) * (GELU_A + 3.0 * GELU_A * GELU_B * square)
                g = (go_ref[o, z].astype(f32) * slope).astype(bf16)
                halves.append(g)
                turn_ref[pl.ds(o * 256 + z * SIDE, SIDE), :] = g.astype(f32)
            r = dot(ex2_ref[...], jnp.concatenate(halves, axis=1))
            r = r[:16] + r[16:]
            g_ref[pl.ds(o, 16, stride=2 * OWN), :] = r[:, :SIDE]
            g_ref[pl.ds(o + OWN, 16, stride=2 * OWN), :] = r[:, SIDE:]
        chunk_copy(out_ref, out_hbm, out_sem, k, size).start()
        return carry

    lax.fori_loop(0, CHUNKS, chunk, 0)
    finish_modes(g_ref, ey2_ref[...], wide_ref, 2 * OWN)
    quarters = [wide_ref[pl.ds(j, 64, stride=4), :][:, : 2 * OWN] for j in range(4)]
    modes_ref[...] = jnp.concatenate(quarters, axis=1)

    def turn(part, carry):
        for z in range(2):
            for u in range(STRIP):
                x = part * STRIP + u
                row = turn_ref[pl.ds(z * SIDE + x, OWN, stride=2 * SIDE), :].astype(bf16)
                gt_ref[z, x] = row
                (first_ref, last_ref)[z][x] = row
        return carry

    lax.fori_loop(0, STRIPS, turn, 0)
    for k in range(CHUNKS):
        chunk_copy(out_ref, out_hbm, out_sem, k, size).wait()


OWN_FIELD = (OWN, 2, SIDE, SIDE)


def middle(conv_int, from_low, from_high, slab, grad_out, tables):
    ex2, ey2, ext3, eyh, eyl = tables
    halo = ((SIDE, OWN, SIDE), bf16, None)
    return whole(
        middle_kernel, ("hbm", "hbm", "vmem", "vmem", None, None, None, None, None, None),
        ((OWN_FIELD, bf16, "hbm"), ((2, SIDE, OWN, SIDE), bf16, None), halo, halo, ((64, SIDE), f32, None)),
        [
            pltpu.VMEM(OWN_FIELD, bf16),
            pltpu.VMEM(OWN_FIELD, bf16),
            pltpu.VMEM(OWN_FIELD, bf16),
            pltpu.VMEM((OWN * 2 * 16, SIDE), f32),
            pltpu.VMEM((16 * 2 * OWN, SIDE), f32),
            pltpu.VMEM((OWN * 2 * SIDE, SIDE), f32),
            pltpu.VMEM((256, SIDE), f32),
            pltpu.SemaphoreType.DMA((CHUNKS,)),
            pltpu.SemaphoreType.DMA((CHUNKS,)),
            pltpu.SemaphoreType.DMA((CHUNKS,)),
        ],
        conv_int, grad_out, from_low, from_high, slab, ex2, ey2, ext3, eyh, eyl,
    )


def kernel_grad_kernel(xt_ref, gt_ref, gl_ref, gh_ref, out_ref, field_ref, sum_ref, sems):
    fetch([xt_ref], [field_ref], sems)
    step = pl.program_id(0)
    lefts, rights = [], []
    for u in range(STRIP):
        x = step * STRIP + u
        near = ((x + SIDE - 1) % SIDE, x, (x + 1) % SIDE)
        for z in range(2):
            lefts.append(jnp.concatenate([field_ref[z, n] for n in near], axis=0))
        planes = []
        for g in (gl_ref[u], gt_ref[0, u], gt_ref[1, u], gh_ref[u]):
            wide = g.astype(f32)
            planes.append((
                pltpu.roll(wide, SIDE - 1, axis=1).astype(bf16),
                g,
                pltpu.roll(wide, 1, axis=1).astype(bf16),
            ))
        for z in range(2):
            rights.append(jnp.concatenate([planes[z - a + 2][c] for a in range(3) for c in range(3)], axis=0))
    part = dot_nt(jnp.concatenate(rights, axis=1), jnp.concatenate(lefts, axis=1))

    @pl.when(step == 0)
    def _():
        sum_ref[...] = part

    @pl.when(step > 0)
    def _():
        sum_ref[...] += part

    @pl.when(step == STRIPS - 1)
    def _():
        tiles = []
        for offset in range(27):
            row = (offset // 9 * 3 + offset % 3) * OWN
            b = offset // 3 % 3
            tile = sum_ref[row : row + OWN, b * ALL : (b + 1) * ALL]
            tiles.append(jnp.concatenate([tile[:8], tile[8:]], axis=1))
        tiles.append(jnp.zeros((8, SIDE), f32))
        for n in range(14):
            out_ref[n * 16 : (n + 1) * 16, :] = jnp.concatenate(tiles[2 * n : 2 * n + 2], axis=0).astype(bf16)


def kernel_grad(xt, gt, gl, gh):
    halo = ((STRIP, OWN, SIDE), lambda k: (k, 0, 0))
    return call(
        kernel_grad_kernel, STRIPS,
        ("hbm", ((2, STRIP, OWN, SIDE), lambda k: (0, k, 0, 0)), halo, halo),
        (((14 * 16, SIDE), bf16, None),),
        [
            pltpu.VMEM((2, SIDE, ALL, SIDE), bf16),
            pltpu.VMEM((9 * OWN, 3 * ALL), f32),
            pltpu.SemaphoreType.DMA((1, STRIPS)),
        ],
        xt, gt, gl, gh,
    )


def last_kernel(
    int_hbm, fl_ref, fh_ref, s_ref, ext3_ref, eyh_ref, eyl_ref, out_hbm, int_ref, out_ref, t_ref, in_sem, out_sem
):
    size = OWN // CHUNKS
    for k in range(CHUNKS):
        chunk_copy(int_hbm, int_ref, in_sem, k, size).start()
    along_y(s_ref, eyh_ref, eyl_ref, t_ref)

    def chunk(k, carry):
        chunk_copy(int_hbm, int_ref, in_sem, k, size).wait()
        for u in range(size):
            o = k * size + u
            smooth = along_x(t_ref, ext3_ref[...], o)
            for z in range(2):
                rim = (fl_ref if z == 0 else fh_ref)[o].astype(f32)
                total = int_ref[o, z].astype(f32) + rim + smooth[:, z * SIDE : (z + 1) * SIDE]
                out_ref[o, z] = total.astype(bf16)
        chunk_copy(out_ref, out_hbm, out_sem, k, size).start()
        return carry

    lax.fori_loop(0, CHUNKS, chunk, 0)
    for k in range(CHUNKS):
        chunk_copy(out_ref, out_hbm, out_sem, k, size).wait()


def last(conv_int, from_low, from_high, slab, tables):
    _, _, ext3, eyh, eyl = tables
    return whole(
        last_kernel, ("hbm", "vmem", "vmem", None, None, None, None), ((OWN_FIELD, bf16, "hbm"),),
        [
            pltpu.VMEM(OWN_FIELD, bf16),
            pltpu.VMEM(OWN_FIELD, bf16),
            pltpu.VMEM((OWN * 2 * 16, SIDE), f32),
            pltpu.SemaphoreType.DMA((CHUNKS,)),
            pltpu.SemaphoreType.DMA((CHUNKS,)),
        ],
        conv_int, from_low, from_high, slab, ext3, eyh, eyl,
    )


def ring(axis, step):
    count = lax.axis_size(axis)
    return [(i, (i + step) % count) for i in range(count)]


def swap(value, bits):
    count = lax.axis_size("col")
    return lax.ppermute(value, "col", [(i, i ^ bits) for i in range(count)])


def exchange(value):
    return lax.all_to_all(value, "gz", 0, 0, tiled=True)


def columns_of(mixed, table_z, groups):
    columns = jnp.einsum("jz,cjm->zcm", table_z, mixed, precision=highest)
    return columns.reshape(groups, -1, SIDE)


def step(features, grad_out, conv_weight, spectral_weight):
    plane_count = features.shape[1]
    groups = lax.axis_size("gz")
    table_x = basis(SIDE, 16)
    table_y = basis(SIDE, 16)
    table_z = basis(plane_count * groups, 16)
    exh, exl = host_split(table_x)
    eyh, eyl = host_split(table_y)
    ex2 = np.concatenate([exh, exl], axis=0)
    ey2 = np.concatenate([eyh, eyh], axis=1)
    ext3 = np.concatenate([exh.T, exl.T, exh.T], axis=1)
    eyh, eyl = (np.repeat(t.reshape(2, 1, 8, SIDE), OWN, axis=1).reshape(256, SIDE) for t in (eyh, eyl))
    tables = (ex2, ey2, ext3, eyh, eyl)

    kernel = conv_weight.reshape(OWN, ALL, 3, 3, 3)
    w_forward = jnp.transpose(kernel, (2, 4, 0, 3, 1)).reshape(9 * OWN, 3 * ALL)
    pieces = jnp.stack([conv_weight] + [swap(conv_weight, bits) for bits in range(1, 4)])
    back = lax.dynamic_slice_in_dim(pieces, lax.axis_index("col") * OWN, OWN, 2)
    back = back.reshape(4, OWN, OWN, 3, 3, 3)
    w_back = jnp.transpose(back, (3, 5, 2, 4, 0, 1)).reshape(9 * OWN, 3 * ALL)

    planes = analyse(features, ex2, ey2)
    planes = exchange(planes.reshape(groups, 8, 2 * ALL))
    xt, conv_int, rim_low, rim_high = front(features, w_forward)
    up, down = ring("gz", 1), ring("gz", -1)
    from_low = lax.ppermute(rim_high, "gz", up)
    from_high = lax.ppermute(rim_low, "gz", down)

    table_gz = table_z.reshape(16, groups, plane_count)
    spectrum = jnp.einsum(
        "jgz,gmzc->cjm", table_gz, planes.reshape(groups, 8, plane_count, ALL), precision=highest
    )
    weights32 = spectral_weight.astype(f32)
    mixed = jnp.sum(weights32 * spectrum[:, None], axis=0)
    slab = exchange(columns_of(mixed, table_z, groups)).reshape(2 * groups, SIDE)
    conv_int, w_back = lax.optimization_barrier((conv_int, w_back))
    layer_out, gt, gt_first, gt_last, grad_planes = middle(conv_int, from_low, from_high, slab, grad_out, tables)

    g_low = lax.ppermute(gt_last, "gz", up)
    g_high = lax.ppermute(gt_first, "gz", down)
    g1 = swap(gt, 1)
    g2 = swap(gt, 2)
    local_grad = kernel_grad(xt, gt, g_low, g_high)
    local_grad = local_grad.reshape(groups, -1, SIDE)
    packed = jnp.concatenate([grad_planes.astype(bf16).reshape(groups, 2, SIDE), local_grad], axis=1)
    packed = exchange(packed)
    scaling = 1.0 / math.sqrt(SIDE * SIDE * plane_count * groups)
    grad_chunk = packed[:, 2:].astype(f32).sum(axis=0) * scaling
    grad_planes = packed[:, :2].astype(f32).reshape(groups, 2, 4, plane_count, OWN)
    g3 = swap(g2, 1)
    grad_modes = jnp.einsum("jgz,grmzc->cjrm", table_gz, grad_planes, precision=highest)
    grad_modes = grad_modes.reshape(OWN, 16, 8)
    back_terms = jnp.sum(weights32 * grad_modes[None], axis=1)
    first = lax.axis_index("col") * OWN
    back_modes = lax.dynamic_slice_in_dim(back_terms, first, OWN, 0)
    for bits in range(1, 4):
        there = jnp.bitwise_xor(lax.axis_index("col"), bits) * OWN
        back_modes = back_modes + swap(lax.dynamic_slice_in_dim(back_terms, there, OWN, 0), bits)
    back_int, back_low, back_high = back_conv((gt, g1, g2, g3), w_back)
    back_from_low = lax.ppermute(back_high, "gz", up)
    back_from_high = lax.ppermute(back_low, "gz", down)
    grad_spectral = spectrum[:, None] * grad_modes[None]

    columns = columns_of(back_modes, table_z, groups).astype(bf16)
    grad_chunk = jnp.broadcast_to(grad_chunk.astype(bf16), (groups, *grad_chunk.shape))
    packed = exchange(jnp.concatenate([columns, grad_chunk], axis=1))
    slab = packed[:, :2].astype(f32).reshape(2 * groups, SIDE)
    grad_input = last(back_int, back_from_low, back_from_high, slab, tables)

    kernel_sum = packed[:, 2:].astype(f32).reshape(28, 8, 2, ALL)[:27]
    grad_conv = jnp.transpose(kernel_sum, (2, 1, 3, 0)).reshape(OWN, ALL, 27)
    return (layer_out, grad_input, grad_conv, grad_spectral)


def solution(mesh):
    return jax.shard_map(
        step,
        mesh=mesh,
        in_specs=(
            P(None, "gz", None, None),
            P("col", "gz", None, None),
            P("col", None, None),
            P(None, "col", None, "gz"),
        ),
        out_specs=(
            P("col", "gz", None, None),
            P("col", "gz", None, None),
            P("col", None, None),
            P(None, "col", None, "gz"),
        ),
        check_vma=False,
    )
```

time: 888 us -> 150 us (0.17); the launches traced: 872 us -> 149 us
  matrix products: 354 us -> 0.99 us
  local copies, waits for them, and re-layouts: 247 us -> 9.1 us
  other arithmetic: 109 us -> 2.84 us
  blocking collectives: 105 us -> 12.4 us
  starting transfers between devices: 9.52 us -> 57 us
  Pallas kernels: 0 us -> 43.7 us
  between operations: 16.2 us -> 1.25 us
  waiting for transfers between devices: 31.4 us -> 21.7 us
    transpose x1 -> x0, matrix products: 234 us -> none  [local(): jnp.transpose(local_grad, (1, 0, 2, 3, 4))]
    broadcast_in_dim x4 -> x1, local copies, waits for them, and re-layouts: 109 us -> 0.01 us  [step(): jnp.broadcast_to(grad_chunk.astype(bf16), (groups, *grad_chunk.shape))]
    conv_general_dilated x2 -> x0, matrix products: 101 us -> none  [correlate(): lax.conv_general_dilated(padded[None], kernel, (1, 1, 1), 'VALID', dimens...]
    broadcast_in_dim x3 -> x0, other arithmetic: 92.5 us -> none  [the longest x2 50.1 us: correlate(): padded[None]]
    all_to_all x6 -> x1, blocking collectives: 105 us -> 12.4 us  [exchange(): return lax.all_to_all(value, 'gz', 0, 0, tiled=True)]
    conv_general_dilated x8 -> x0, local copies, waits for them, and re-layouts: 90.7 us -> none  [correlate(): lax.conv_general_dilated(padded[None], kernel, (1, 1, 1), 'VALID', dimens...]
    pallas_call x0 -> x6, Pallas kernels: none -> 43.7 us  [the longest x3 29.9 us: call(): pl.pallas_call(kernel, grid=(grid,), in_specs=[spec(entry, value.shape) f...]
    reduce_scatter x1 -> x0, waiting for transfers between devices: 31.4 us -> none  [local(): lax.psum_scatter(contributions, 'col', scatter_dimension=0, tiled=True)]
  transfers between devices with their start and end apart: 6 -> 18, of which waited for: 1 -> 5; matrix products, arithmetic and copies ran while one was open for 57% -> 7% of each run, Pallas kernels for 0% -> 17%
where the time goes in v2:
time: 150 us; the launch traced here: 149 us
  starting transfers between devices  57 us (38%)
  Pallas kernels  43.7 us (29%)
  waiting for transfers between devices  21.7 us (14%)
  blocking collectives  12.4 us (8%)
  local copies, waits for them, and re-layouts  9.1 us (6%)
  other arithmetic  2.84 us (2%)
    pallas_call x3, Pallas kernels, call(): pl.pallas_call(kernel, grid=(grid,), in_specs=[spec(entry, value.shape) f...  29.9 us
    ppermute x9, starting transfers between devices, swap(): return lax.ppermute(value, 'col', [(i, i ^ bits) for i in range(count)])  20.6 us
    all_to_all x3, starting transfers between devices, exchange(): return lax.all_to_all(value, 'gz', 0, 0, tiled=True)  19.3 us
    pallas_call x3, Pallas kernels, whole(): pl.pallas_call(kernel, in_specs=[spec(kind) for kind in ins], out_specs=t...  13.8 us
    all_to_all x1, blocking collectives, exchange(): return lax.all_to_all(value, 'gz', 0, 0, tiled=True)  12.4 us
    ppermute x1, waiting for transfers between devices, step(): g_low = lax.ppermute(gt_last, 'gz', up)  9.46 us
    all_to_all x3, waiting for transfers between devices, exchange(): return lax.all_to_all(value, 'gz', 0, 0, tiled=True)  8.94 us
    ppermute x1, starting transfers between devices, step(): back_from_high = lax.ppermute(back_low, 'gz', down)  5.44 us
  transfers between devices with their start and end apart: 18, of which 5 were waited for; matrix products, arithmetic and copies ran while one was open for 7% of the time, Pallas kernels for 17%

profile of v2, /device:TPU:1, one launch (start us, length us, event | category | flops | bytes accessed | tf_op | source)
XLA Modules:
  0.0 149.0 jit_solution(1548302876831529869)
XLA Ops:
  0.6 1.5 collective-permute-start
  2.1 3.0 %collective-permute-start.1 = (bf16[16,64,27]{1,0,2:T(8,128)(2,1)}, bf16[16,64,27]{1,0,2:T(8,128)(2,1)S(1)}, u32[]{:S(2)}, u32[]{:S(2)}) collective-permute-start(bf16[16,64,27]{1,0,2:T(8,128)(2,1)} %param.15), channel_id=1, source_target_pairs={{0,2},{1,3},{2,0},{3,1},{4,6},{5,7},{6,4},{7,5},{8,10},{9,11},{10,... | collective-permute-start | bytes 165896 | tf_op jit(solution)/shard_map/ppermute | solution.py:486
  5.1 0.2 collective-permute-start.2
  5.3 0.7 copy-done.4
  6.0 0.7 copy-done.6
  6.7 3.7 %shard_map.157 = f32[256,128]{1,0:T(8,128)} custom-call(bf16[64,2,128,128]{3,2,1,0:T(8,128)(2,1)} %f_hbm.1, bf16[32,128]{1,0:T(8,128)(2,1)S(1)} %copy-done.4, bf16[16,256]{1,0:T(8,128)(2,1)S(1)} %copy-done.6), custom_call_target="tpu_custom_call" | custom-call | flops 1811939328 | bytes 8388608 | tf_op jit(solution)/shard_map/pallas_call | solution.py:68
  10.4 9.1 %all-to-all-start = ((f32[32,8,128]{2,1,0:T(8,128)}), f32[32,8,128]{2,1,0:T(8,128)S(1)}, u32[]{:S(2)}, u32[]{:S(2)}) async-start(f32[32,8,128]{2,1,0:T(8,128)} %bitcast.9), calls=%async_computation | async-start | bytes 262144 | tf_op jit(solution)/shard_map/all_to_all | solution.py:490
  19.7 0.8 reshape.61.w_ref
  20.4 11.7 %shard_map.156 = (bf16[2,128,64,128]{3,2,1,0:T(8,128)(2,1)}, bf16[16,2,128,128]{3,2,1,0:T(8,128)(2,1)}, bf16[16,128,128]{2,1,0:T(8,128)(2,1)}, bf16[16,128,128]{2,1,0:T(8,128)(2,1)}) custom-call(bf16[64,2,128,128]{3,2,1,0:T(8,128)(2,1)} %f_hbm.1, bf16[144,192]{1,0:T(8,128)(2,1)} %reshape.61.w_ref), custom_call_target="tpu_custom_call" | custom-call | flops 1811939328 | bytes 8388608 | tf_op jit(solution)/shard_map/pallas_call | solution.py:47
  32.1 1.3 collective-permute-start.3
  33.4 4.5 %collective-permute-start.4 = (bf16[16,128,128]{2,1,0:T(8,128)(2,1)}, bf16[16,128,128]{2,1,0:T(8,128)(2,1)S(1)}, u32[]{:S(2)}, u32[]{:S(2)}) collective-permute-start(bf16[16,128,128]{2,1,0:T(8,128)(2,1)} %get-tuple-element.21), channel_id=1, source_target_pairs={{0,124},{4,0},{8,4},{12,8},{16,12},{20,16},{24,20},{28,24},{32,28}... | collective-permute-start | bytes 1572872 | tf_op jit(solution)/shard_map/ppermute | solution.py:524
  38.1 0.3 convolution_bitcast_fusion
  38.5 0.3 fusion.1
  39.1 0.3 copy.44
  39.4 0.9 reshape.66
  40.3 3.9 %all-to-all-start.1 = ((f32[32,2,128]{2,1,0:T(2,128)}), f32[32,2,128]{2,1,0:T(2,128)S(1)}, u32[]{:S(2)}, u32[]{:S(2)}) async-start(f32[32,2,128]{2,1,0:T(2,128)} %reshape.66), calls=%async_computation.1 | async-start | bytes 65536 | tf_op jit(solution)/shard_map/all_to_all | solution.py:490
  44.2 0.2 dynamic-slice_maximum_fusion
  44.4 0.3 copy.40
  44.7 0.9 reshape.63.w_ref
  45.6 5.8 %all-to-all-done.1 = f32[32,2,128]{2,1,0:T(2,128)S(1)} async-done(((f32[32,2,128]{2,1,0:T(2,128)}), f32[32,2,128]{2,1,0:T(2,128)S(1)}, u32[]{:S(2)}, u32[]{:S(2)}) %all-to-all-start.1) | async-done | bytes 32800 | tf_op jit(solution)/shard_map/all_to_all | solution.py:490
  51.4 7.1 %shard_map.158 = (bf16[16,2,128,128]{3,2,1,0:T(8,128)(2,1)}, bf16[2,128,16,128]{3,2,1,0:T(8,128)(2,1)S(1)}, bf16[128,16,128]{2,1,0:T(8,128)(2,1)S(1)}, bf16[128,16,128]{2,1,0:T(8,128)(2,1)S(1)}, f32[64,128]{1,0:T(8,128)S(1)}) custom-call(bf16[16,2,128,128]{3,2,1,0:T(8,128)(2,1)} %get-tuple-element.19.int_hbm, bf16[16,2,128,128]{3,2,1,0:T(8,128)(2,1)} %go_hbm.1, ...), custom_call_target="tpu_custom_call" | custom-call | flops 1811939328 | bytes 8388608 | tf_op jit(solution)/shard_map/pallas_call | solution.py:68
  58.6 2.7 %collective-permute-start.6 = (bf16[2,128,16,128]{3,2,1,0:T(8,128)(2,1)S(1)}, bf16[2,128,16,128]{3,2,1,0:T(8,128)(2,1)S(1)}, u32[]{:S(2)}, u32[]{:S(2)}) collective-permute-start(bf16[2,128,16,128]{3,2,1,0:T(8,128)(2,1)S(1)} %get-tuple-element.23.g0.gt_ref), channel_id=1, source_target_pairs={{0,2},{1,3},{2,0},{3,1},{4,6},{5,7},{6,4},{7,5},{8,10},{9,11},{10,... | collective-permute-start | bytes 3145736 | tf_op jit(solution)/shard_map/ppermute | solution.py:486
  61.3 0.3 collective-permute-start.10
  61.6 5.4 %collective-permute-start.11 = (bf16[128,16,128]{2,1,0:T(8,128)(2,1)S(1)}, bf16[128,16,128]{2,1,0:T(8,128)(2,1)S(1)}, u32[]{:S(2)}, u32[]{:S(2)}) collective-permute-start(bf16[128,16,128]{2,1,0:T(8,128)(2,1)S(1)} %get-tuple-element.31), channel_id=1, source_target_pairs={{0,124},{4,0},{8,4},{12,8},{16,12},{20,16},{24,20},{28,24},{32,28}... | collective-permute-start | bytes 1572872 | tf_op jit(solution)/shard_map/ppermute | solution.py:537
  67.0 9.5 %collective-permute-done.10.gl_ref = bf16[128,16,128]{2,1,0:T(8,128)(2,1)S(1)} collective-permute-done((bf16[128,16,128]{2,1,0:T(8,128)(2,1)S(1)}, bf16[128,16,128]{2,1,0:T(8,128)(2,1)S(1)}, u32[]{:S(2)}, u32[]{:S(2)}) %collective-permute-start.10) | collective-permute-done | bytes 524320 | tf_op jit(solution)/shard_map/ppermute | solution.py:536
  76.5 0.8 copy-done.14
  77.3 0.8 copy-done.15
  78.1 9.6 %shard_map.160 = bf16[224,128]{1,0:T(8,128)(2,1)} custom-call(bf16[2,128,64,128]{3,2,1,0:T(8,128)(2,1)} %get-tuple-element.29.xt_ref, bf16[2,128,16,128]{3,2,1,0:T(8,128)(2,1)} %copy-done, bf16[128,16,128]{2,1,0:T(8,128)(2,1)} %copy-done.14, bf16[128,16,128]{2,1,0:T(8,128)(2,1)} %copy-done.15), custom_call_target="tpu_custom_call" | custom-call | flops 1811939328 | bytes 8388608 | tf_op jit(solution)/shard_map/pallas_call | solution.py:47
  87.7 0.8 reshape.69
  88.6 0.7 pad_maximum_fusion
  89.3 6.3 %all-to-all-start.2 = ((bf16[32,9,128]{2,1,0:T(8,128)(2,1)}), bf16[32,9,128]{2,1,0:T(8,128)(2,1)S(1)}, u32[]{:S(2)}, u32[]{:S(2)}) async-start(bf16[32,9,128]{2,1,0:T(8,128)(2,1)} %pad_maximum_fusion), calls=%async_computation.2 | async-start | bytes 262144 | tf_op jit(solution)/shard_map/all_to_all | solution.py:490
  95.6 4.1 %collective-permute-start.5 = (bf16[2,128,16,128]{3,2,1,0:T(8,128)(2,1)}, bf16[2,128,16,128]{3,2,1,0:T(8,128)(2,1)}, u32[]{:S(2)}, u32[]{:S(2)}) collective-permute-start(bf16[2,128,16,128]{3,2,1,0:T(8,128)(2,1)} %copy-done), channel_id=1, source_target_pairs={{0,1},{1,0},{2,3},{3,2},{4,5},{5,4},{6,7},{7,6},{8,9},{9,8},{10,11... | collective-permute-start | bytes 3145736 | tf_op jit(solution)/shard_map/ppermute | solution.py:486
  99.7 3.1 %all-to-all-done.2 = bf16[32,9,128]{2,1,0:T(8,128)(2,1)S(1)} async-done(((bf16[32,9,128]{2,1,0:T(8,128)(2,1)}), bf16[32,9,128]{2,1,0:T(8,128)(2,1)S(1)}, u32[]{:S(2)}, u32[]{:S(2)}) %all-to-all-start.2) | async-done | bytes 73760 | tf_op jit(solution)/shard_map/all_to_all | solution.py:490
  103.0 5.3 %collective-permute-start.7 = (bf16[2,128,16,128]{3,2,1,0:T(8,128)(2,1)S(1)}, bf16[2,128,16,128]{3,2,1,0:T(8,128)(2,1)}, u32[]{:S(2)}, u32[]{:S(2)}) collective-permute-start(bf16[2,128,16,128]{3,2,1,0:T(8,128)(2,1)S(1)} %collective-permute-done.6.g2), channel_id=1, source_target_pairs={{0,1},{1,0},{2,3},{3,2},{4,5},{5,4},{6,7},{7,6},{8,9},{9,8},{10,11... | collective-permute-start | bytes 3145736 | tf_op jit(solution)/shard_map/ppermute | solution.py:486
  108.6 1.3 broadcast_multiply_fusion
  110.2 0.4 collective-permute-start.13
  110.6 3.2 %collective-permute-start.14 = (f32[16,16,8]{0,2,1:T(8,128)S(1)}, f32[16,16,8]{0,2,1:T(8,128)S(1)}, u32[]{:S(2)}, u32[]{:S(2)}) collective-permute-start(f32[16,16,8]{0,2,1:T(8,128)S(1)} %get-tuple-element.35), channel_id=1, source_target_pairs={{0,3},{1,2},{2,1},{3,0},{4,7},{5,6},{6,5},{7,4},{8,11},{9,10},{10,... | collective-permute-start | bytes 24584 | tf_op jit(solution)/shard_map/ppermute | solution.py:486
  113.8 1.0 collective-permute-done.13
  114.9 2.3 %collective-permute-done.14 = f32[16,16,8]{0,2,1:T(8,128)S(1)} collective-permute-done((f32[16,16,8]{0,2,1:T(8,128)S(1)}, f32[16,16,8]{0,2,1:T(8,128)S(1)}, u32[]{:S(2)}, u32[]{:S(2)}) %collective-permute-start.14) | collective-permute-done | bytes 8224 | tf_op jit(solution)/shard_map/ppermute | solution.py:486
  117.3 8.6 %shard_map.159 = (bf16[16,2,128,128]{3,2,1,0:T(8,128)(2,1)}, bf16[16,128,128]{2,1,0:T(8,128)(2,1)}, bf16[16,128,128]{2,1,0:T(8,128)(2,1)}) custom-call(bf16[2,128,16,128]{3,2,1,0:T(8,128)(2,1)} %copy-done, bf16[2,128,16,128]{3,2,1,0:T(8,128)(2,1)} %collective-permute-done.5.g1, bf16[2,128,16,128]{3,2,1,0:T(8,128)(2,1)} %copy-done.13, ...), custom_call_target="tpu_custom_call" | custom-call | flops 1811939328 | bytes 8388608 | tf_op jit(solution)/shard_map/pallas_call | solution.py:47
  125.8 0.3 collective-permute-start.8
  126.2 5.4 %collective-permute-start.9 = (bf16[16,128,128]{2,1,0:T(8,128)(2,1)}, bf16[16,128,128]{2,1,0:T(8,128)(2,1)S(1)}, u32[]{:S(2)}, u32[]{:S(2)}) collective-permute-start(bf16[16,128,128]{2,1,0:T(8,128)(2,1)} %get-tuple-element.27), channel_id=1, source_target_pairs={{0,124},{4,0},{8,4},{12,8},{16,12},{20,16},{24,20},{28,24},{32,28}... | collective-permute-start | bytes 1572872 | tf_op jit(solution)/shard_map/ppermute | solution.py:558
  131.6 0.3 fusion
  131.9 0.3 copy.48
  132.2 0.2 convert_element_type.28
  132.5 12.4 %all_to_all.20 = bf16[32,9,128]{2,1,0:T(8,128)(2,1)S(1)} all-to-all(bf16[32,9,128]{2,1,0:T(8,128)(2,1)S(1)} %pad_maximum_fusion.1), channel_id=1, replica_groups=mesh['gz'=32,'col'=4] {'gz'}, dimensions={0} | all-to-all | bytes 147456 | tf_op jit(solution)/shard_map/all_to_all | solution.py:490
  145.2 0.7 copy.59
  145.9 3.0 %shard_map.161 = bf16[16,2,128,128]{3,2,1,0:T(8,128)(2,1)} custom-call(bf16[16,2,128,128]{3,2,1,0:T(8,128)(2,1)} %get-tuple-element.25.int_hbm, bf16[16,128,128]{2,1,0:T(8,128)(2,1)S(1)} %collective-permute-done.8.fl_ref, bf16[16,128,128]{2,1,0:T(8,128)(2,1)S(1)} %collective-permute-done.9.fh_ref, f32[64,128]{1,0:T(8,128)S(1)} %convert.5.s_ref, ...), custom_call_target="tpu_custom_call" | custom-call | flops 1811939328 | bytes 8388608 | tf_op jit(solution)/shard_map/pallas_call | solution.py:68
  (63 shorter events, 1.7 us)
Async XLA Ops:
  0.6 43.6 %collective-permute-start = (bf16[16,64,27]{1,0,2:T(8,128)(2,1)}, bf16[16,64,27]{1,0,2:T(8,128)(2,1)S(1)}, u32[]{:S(2)}, u32[]{:S(2)}) collective-permute-start(bf16[16,64,27]{1,0,2:T(8,128)(2,1)} %param.15), channel_id=1, source_target_pairs={{0,1},{1,0},{2,3},{3,2},{4,5},{5,4},{6,7},{7,6},{8,9},{9,8},{10,11... | collective-permute-start | bytes 165896 | tf_op jit(solution)/shard_map/ppermute | solution.py:486
  2.1 42.1 %collective-permute-start.1 = (bf16[16,64,27]{1,0,2:T(8,128)(2,1)}, bf16[16,64,27]{1,0,2:T(8,128)(2,1)S(1)}, u32[]{:S(2)}, u32[]{:S(2)}) collective-permute-start(bf16[16,64,27]{1,0,2:T(8,128)(2,1)} %param.15), channel_id=1, source_target_pairs={{0,2},{1,3},{2,0},{3,1},{4,6},{5,7},{6,4},{7,5},{8,10},{9,11},{10,... | collective-permute-start | bytes 165896 | tf_op jit(solution)/shard_map/ppermute | solution.py:486
  5.1 39.1 %collective-permute-start.2 = (bf16[16,64,27]{1,0,2:T(8,128)(2,1)}, bf16[16,64,27]{1,0,2:T(8,128)(2,1)S(1)}, u32[]{:S(2)}, u32[]{:S(2)}) collective-permute-start(bf16[16,64,27]{1,0,2:T(8,128)(2,1)} %param.15), channel_id=1, source_target_pairs={{0,3},{1,2},{2,1},{3,0},{4,7},{5,6},{6,5},{7,4},{8,11},{9,10},{10,... | collective-permute-start | bytes 165896 | tf_op jit(solution)/shard_map/ppermute | solution.py:486
  5.3 0.7 copy-start.4
  6.0 0.7 copy-start.6
  6.7 12.9 %copy-start.9 = (bf16[16,64,27]{1,0,2:T(8,128)(2,1)S(1)}, bf16[16,64,27]{1,0,2:T(8,128)(2,1)}, u32[]{:S(2)}) copy-start(bf16[16,64,27]{1,0,2:T(8,128)(2,1)} %param.15) | copy-start | bytes 165892
  10.4 27.7 %copy-start.12 = (f32[16,32,2,1]{1,0,2,3:T(8,128)S(1)}, f32[16,32,2,1]{1,0,2,3:T(8,128)}, u32[]{:S(2)}) copy-start(f32[16,32,2,1]{1,0,2,3:T(8,128)} %constant.45) | copy-start | bytes 12292
  10.4 28.1 %copy-start.8 = (bf16[64,16,16,8]{0,3,2,1:T(8,128)(2,1)S(1)}, bf16[64,16,16,8]{0,3,2,1:T(8,128)(2,1)}, u32[]{:S(2)}) copy-start(bf16[64,16,16,8]{0,3,2,1:T(8,128)(2,1)} %param.16) | copy-start | bytes 786436
  10.4 27.5 %all-to-all-start = ((f32[32,8,128]{2,1,0:T(8,128)}), f32[32,8,128]{2,1,0:T(8,128)S(1)}, u32[]{:S(2)}, u32[]{:S(2)}) async-start(f32[32,8,128]{2,1,0:T(8,128)} %bitcast.9), calls=%async_computation | async-start | bytes 262144 | tf_op jit(solution)/shard_map/all_to_all | solution.py:490
  20.4 18.5 %copy-start.10 = (f32[16,64,1]{1,0,2:T(8,128)S(1)}, f32[16,64,1]{1,0,2:T(8,128)}, u32[]{:S(2)}) copy-start(f32[16,64,1]{1,0,2:T(8,128)} %constant.44) | copy-start | bytes 12292
  32.1 19.3 %copy-start.1 = (bf16[256,128]{1,0:T(8,128)(2,1)S(1)}, bf16[256,128]{1,0:T(8,128)(2,1)}, u32[]{:S(2)}) copy-start(bf16[256,128]{1,0:T(8,128)(2,1)} %constant.39.clone.eyh_ref) | copy-start | bytes 196612
  32.1 19.3 %copy-start.2 = (bf16[256,128]{1,0:T(8,128)(2,1)S(1)}, bf16[256,128]{1,0:T(8,128)(2,1)}, u32[]{:S(2)}) copy-start(bf16[256,128]{1,0:T(8,128)(2,1)} %constant.40.clone.eyl_ref) | copy-start | bytes 196612
  32.1 19.3 %copy-start.3 = (bf16[128,48]{1,0:T(8,128)(2,1)S(1)}, bf16[128,48]{1,0:T(8,128)(2,1)}, u32[]{:S(2)}) copy-start(bf16[128,48]{1,0:T(8,128)(2,1)} %constant.38.clone.ext3_ref) | copy-start | bytes 36868
  32.1 19.3 %copy-start.5 = (bf16[32,128]{1,0:T(8,128)(2,1)S(1)}, bf16[32,128]{1,0:T(8,128)(2,1)}, u32[]{:S(2)}) copy-start(bf16[32,128]{1,0:T(8,128)(2,1)} %constant.34.clone.ex2_ref) | copy-start | bytes 24580
  32.1 19.3 %copy-start.7 = (bf16[16,256]{1,0:T(8,128)(2,1)S(1)}, bf16[16,256]{1,0:T(8,128)(2,1)}, u32[]{:S(2)}) copy-start(bf16[16,256]{1,0:T(8,128)(2,1)} %constant.35.clone.ey2_ref) | copy-start | bytes 24580
  32.1 19.2 %collective-permute-start.3 = (bf16[16,128,128]{2,1,0:T(8,128)(2,1)}, bf16[16,128,128]{2,1,0:T(8,128)(2,1)S(1)}, u32[]{:S(2)}, u32[]{:S(2)}) collective-permute-start(bf16[16,128,128]{2,1,0:T(8,128)(2,1)} %get-tuple-element.20), channel_id=1, source_target_pairs={{0,4},{4,8},{8,12},{12,16},{16,20},{20,24},{24,28},{28,32},{32,36}... | collective-permute-start | bytes 1572872 | tf_op jit(solution)/shard_map/ppermute | solution.py:523
  33.4 18.0 %collective-permute-start.4 = (bf16[16,128,128]{2,1,0:T(8,128)(2,1)}, bf16[16,128,128]{2,1,0:T(8,128)(2,1)S(1)}, u32[]{:S(2)}, u32[]{:S(2)}) collective-permute-start(bf16[16,128,128]{2,1,0:T(8,128)(2,1)} %get-tuple-element.21), channel_id=1, source_target_pairs={{0,124},{4,0},{8,4},{12,8},{16,12},{20,16},{24,20},{28,24},{32,28}... | collective-permute-start | bytes 1572872 | tf_op jit(solution)/shard_map/ppermute | solution.py:524
  40.3 11.0 %all-to-all-start.1 = ((f32[32,2,128]{2,1,0:T(2,128)}), f32[32,2,128]{2,1,0:T(2,128)S(1)}, u32[]{:S(2)}, u32[]{:S(2)}) async-start(f32[32,2,128]{2,1,0:T(2,128)} %reshape.66), calls=%async_computation.1 | async-start | bytes 65536 | tf_op jit(solution)/shard_map/all_to_all | solution.py:490
  58.6 19.5 %copy-start = (bf16[2,128,16,128]{3,2,1,0:T(8,128)(2,1)}, bf16[2,128,16,128]{3,2,1,0:T(8,128)(2,1)S(1)}, u32[]{:S(2)}) copy-start(bf16[2,128,16,128]{3,2,1,0:T(8,128)(2,1)S(1)} %get-tuple-element.23.g0.gt_ref) | copy-start | bytes 3145732
  58.6 49.7 %copy-start.11 = (f32[16,32,2,1,1]{1,0,2,4,3:T(8,128)S(1)}, f32[16,32,2,1,1]{1,0,2,4,3:T(8,128)}, u32[]{:S(2)}) copy-start(f32[16,32,2,1,1]{1,0,2,4,3:T(8,128)} %constant.46) | copy-start | bytes 12292
  58.6 44.4 %collective-permute-start.6 = (bf16[2,128,16,128]{3,2,1,0:T(8,128)(2,1)S(1)}, bf16[2,128,16,128]{3,2,1,0:T(8,128)(2,1)S(1)}, u32[]{:S(2)}, u32[]{:S(2)}) collective-permute-start(bf16[2,128,16,128]{3,2,1,0:T(8,128)(2,1)S(1)} %get-tuple-element.23.g0.gt_ref), channel_id=1, source_target_pairs={{0,2},{1,3},{2,0},{3,1},{4,6},{5,7},{6,4},{7,5},{8,10},{9,11},{10,... | collective-permute-start | bytes 3145736 | tf_op jit(solution)/shard_map/ppermute | solution.py:486
  61.3 15.2 %collective-permute-start.10 = (bf16[128,16,128]{2,1,0:T(8,128)(2,1)S(1)}, bf16[128,16,128]{2,1,0:T(8,128)(2,1)S(1)}, u32[]{:S(2)}, u32[]{:S(2)}) collective-permute-start(bf16[128,16,128]{2,1,0:T(8,128)(2,1)S(1)} %get-tuple-element.30), channel_id=1, source_target_pairs={{0,4},{4,8},{8,12},{12,16},{16,20},{20,24},{24,28},{28,32},{32,36}... | collective-permute-start | bytes 1572872 | tf_op jit(solution)/shard_map/ppermute | solution.py:536
  61.6 14.9 %collective-permute-start.11 = (bf16[128,16,128]{2,1,0:T(8,128)(2,1)S(1)}, bf16[128,16,128]{2,1,0:T(8,128)(2,1)S(1)}, u32[]{:S(2)}, u32[]{:S(2)}) collective-permute-start(bf16[128,16,128]{2,1,0:T(8,128)(2,1)S(1)} %get-tuple-element.31), channel_id=1, source_target_pairs={{0,124},{4,0},{8,4},{12,8},{16,12},{20,16},{24,20},{28,24},{32,28}... | collective-permute-start | bytes 1572872 | tf_op jit(solution)/shard_map/ppermute | solution.py:537
  76.5 0.8 copy-start.14
  77.2 0.8 copy-start.15
  89.3 13.6 %all-to-all-start.2 = ((bf16[32,9,128]{2,1,0:T(8,128)(2,1)}), bf16[32,9,128]{2,1,0:T(8,128)(2,1)S(1)}, u32[]{:S(2)}, u32[]{:S(2)}) async-start(bf16[32,9,128]{2,1,0:T(8,128)(2,1)} %pad_maximum_fusion), calls=%async_computation.2 | async-start | bytes 262144 | tf_op jit(solution)/shard_map/all_to_all | solution.py:490
  95.6 21.7 %collective-permute-start.5 = (bf16[2,128,16,128]{3,2,1,0:T(8,128)(2,1)}, bf16[2,128,16,128]{3,2,1,0:T(8,128)(2,1)}, u32[]{:S(2)}, u32[]{:S(2)}) collective-permute-start(bf16[2,128,16,128]{3,2,1,0:T(8,128)(2,1)} %copy-done), channel_id=1, source_target_pairs={{0,1},{1,0},{2,3},{3,2},{4,5},{5,4},{6,7},{7,6},{8,9},{9,8},{10,11... | collective-permute-start | bytes 3145736 | tf_op jit(solution)/shard_map/ppermute | solution.py:486
  103.0 14.2 %copy-start.13 = (bf16[2,128,16,128]{3,2,1,0:T(8,128)(2,1)}, bf16[2,128,16,128]{3,2,1,0:T(8,128)(2,1)S(1)}, u32[]{:S(2)}) copy-start(bf16[2,128,16,128]{3,2,1,0:T(8,128)(2,1)S(1)} %collective-permute-done.6.g2) | copy-start | bytes 3145732
  103.0 14.2 %collective-permute-start.7 = (bf16[2,128,16,128]{3,2,1,0:T(8,128)(2,1)S(1)}, bf16[2,128,16,128]{3,2,1,0:T(8,128)(2,1)}, u32[]{:S(2)}, u32[]{:S(2)}) collective-permute-start(bf16[2,128,16,128]{3,2,1,0:T(8,128)(2,1)S(1)} %collective-permute-done.6.g2), channel_id=1, source_target_pairs={{0,1},{1,0},{2,3},{3,2},{4,5},{5,4},{6,7},{7,6},{8,9},{9,8},{10,11... | collective-permute-start | bytes 3145736 | tf_op jit(solution)/shard_map/ppermute | solution.py:486
  110.1 3.8 %collective-permute-start.12 = (f32[16,16,8]{0,2,1:T(8,128)S(1)}, f32[16,16,8]{0,2,1:T(8,128)S(1)}, u32[]{:S(2)}, u32[]{:S(2)}) collective-permute-start(f32[16,16,8]{0,2,1:T(8,128)S(1)} %get-tuple-element.34), channel_id=1, source_target_pairs={{0,1},{1,0},{2,3},{3,2},{4,5},{5,4},{6,7},{7,6},{8,9},{9,8},{10,11... | collective-permute-start | bytes 24584 | tf_op jit(solution)/shard_map/ppermute | solution.py:486
  110.2 4.7 %collective-permute-start.13 = (f32[16,16,8]{0,2,1:T(8,128)S(1)}, f32[16,16,8]{0,2,1:T(8,128)S(1)}, u32[]{:S(2)}, u32[]{:S(2)}) collective-permute-start(f32[16,16,8]{0,2,1:T(8,128)S(1)} %get-tuple-element.36), channel_id=1, source_target_pairs={{0,2},{1,3},{2,0},{3,1},{4,6},{5,7},{6,4},{7,5},{8,10},{9,11},{10,... | collective-permute-start | bytes 24584 | tf_op jit(solution)/shard_map/ppermute | solution.py:486
  110.6 6.6 %collective-permute-start.14 = (f32[16,16,8]{0,2,1:T(8,128)S(1)}, f32[16,16,8]{0,2,1:T(8,128)S(1)}, u32[]{:S(2)}, u32[]{:S(2)}) collective-permute-start(f32[16,16,8]{0,2,1:T(8,128)S(1)} %get-tuple-element.35), channel_id=1, source_target_pairs={{0,3},{1,2},{2,1},{3,0},{4,7},{5,6},{6,5},{7,4},{8,11},{9,10},{10,... | collective-permute-start | bytes 24584 | tf_op jit(solution)/shard_map/ppermute | solution.py:486
  125.8 20.0 %collective-permute-start.8 = (bf16[16,128,128]{2,1,0:T(8,128)(2,1)}, bf16[16,128,128]{2,1,0:T(8,128)(2,1)S(1)}, u32[]{:S(2)}, u32[]{:S(2)}) collective-permute-start(bf16[16,128,128]{2,1,0:T(8,128)(2,1)} %get-tuple-element.26), channel_id=1, source_target_pairs={{0,4},{4,8},{8,12},{12,16},{16,20},{20,24},{24,28},{28,32},{32,36}... | collective-permute-start | bytes 1572872 | tf_op jit(solution)/shard_map/ppermute | solution.py:557
  126.2 19.7 %collective-permute-start.9 = (bf16[16,128,128]{2,1,0:T(8,128)(2,1)}, bf16[16,128,128]{2,1,0:T(8,128)(2,1)S(1)}, u32[]{:S(2)}, u32[]{:S(2)}) collective-permute-start(bf16[16,128,128]{2,1,0:T(8,128)(2,1)} %get-tuple-element.27), channel_id=1, source_target_pairs={{0,124},{4,0},{8,4},{12,8},{16,12},{20,16},{24,20},{28,24},{32,28}... | collective-permute-start | bytes 1572872 | tf_op jit(solution)/shard_map/ppermute | solution.py:558

commit v3 on v2

--- a/solution.py
+++ b/solution.py
@@ -7,6 +7,7 @@
 from jax.experimental import pallas as pl
 from jax.experimental.pallas import tpu as pltpu
 from jax.sharding import PartitionSpec as P
+
 
 highest = lax.Precision.HIGHEST
 f32 = jnp.float32
@@ -416,8 +417,8 @@
             b = offset // 3 % 3
             tile = sum_ref[row : row + OWN, b * ALL : (b + 1) * ALL]
             tiles.append(jnp.concatenate([tile[:8], tile[8:]], axis=1))
-        tiles.append(jnp.zeros((8, SIDE), f32))
-        for n in range(14):
+        tiles += [jnp.zeros((8, SIDE), f32)] * 5
+        for n in range(16):
             out_ref[n * 16 : (n + 1) * 16, :] = jnp.concatenate(tiles[2 * n : 2 * n + 2], axis=0).astype(bf16)
 
 
@@ -426,7 +427,7 @@
     return call(
         kernel_grad_kernel, STRIPS,
         ("hbm", ((2, STRIP, OWN, SIDE), lambda k: (0, k, 0, 0)), halo, halo),
-        (((14 * 16, SIDE), bf16, None),),
+        (((32 * 8, SIDE), bf16, None),),
         [
             pltpu.VMEM((2, SIDE, ALL, SIDE), bf16),
             pltpu.VMEM((9 * OWN, 3 * ALL), f32),
@@ -541,6 +542,7 @@
     local_grad = local_grad.reshape(groups, -1, SIDE)
     packed = jnp.concatenate([grad_planes.astype(bf16).reshape(groups, 2, SIDE), local_grad], axis=1)
     packed = exchange(packed)
+    g2, packed = lax.optimization_barrier((g2, packed))
     scaling = 1.0 / math.sqrt(SIDE * SIDE * plane_count * groups)
     grad_chunk = packed[:, 2:].astype(f32).sum(axis=0) * scaling
     grad_planes = packed[:, :2].astype(f32).reshape(groups, 2, 4, plane_count, OWN)
@@ -548,12 +550,14 @@
     grad_modes = jnp.einsum("jgz,grmzc->cjrm", table_gz, grad_planes, precision=highest)
     grad_modes = grad_modes.reshape(OWN, 16, 8)
     back_terms = jnp.sum(weights32 * grad_modes[None], axis=1)
-    first = lax.axis_index("col") * OWN
-    back_modes = lax.dynamic_slice_in_dim(back_terms, first, OWN, 0)
-    for bits in range(1, 4):
-        there = jnp.bitwise_xor(lax.axis_index("col"), bits) * OWN
-        back_modes = back_modes + swap(lax.dynamic_slice_in_dim(back_terms, there, OWN, 0), bits)
+    own = lax.axis_index("col")
+    shares = [
+        lax.dynamic_slice_in_dim(back_terms, jnp.bitwise_xor(own, bits) * OWN, OWN, 0) for bits in range(4)
+    ]
+    shares = [swap(share, bits) if bits else share for bits, share in enumerate(shares)]
     back_int, back_low, back_high = back_conv((gt, g1, g2, g3), w_back)
+    shares, back_low, back_high = lax.optimization_barrier((shares, back_low, back_high))
+    back_modes = sum(shares)
     back_from_low = lax.ppermute(back_high, "gz", up)
     back_from_high = lax.ppermute(back_low, "gz", down)
     grad_spectral = spectrum[:, None] * grad_modes[None]
@@ -564,7 +568,7 @@
     slab = packed[:, :2].astype(f32).reshape(2 * groups, SIDE)
     grad_input = last(back_int, back_from_low, back_from_high, slab, tables)
 
-    kernel_sum = packed[:, 2:].astype(f32).reshape(28, 8, 2, ALL)[:27]
+    kernel_sum = packed[:27, 2:].astype(f32).reshape(27, 8, 2, ALL)
     grad_conv = jnp.transpose(kernel_sum, (2, 1, 3, 0)).reshape(OWN, ALL, 27)
     return (layer_out, grad_input, grad_conv, grad_spectral)
 

time: 150 us -> 147 us (0.980)
  waiting for transfers between devices: 21.7 us -> 18.5 us
    ppermute x9, waiting for transfers between devices: 3.31 us -> 0.02 us  [swap(): return lax.ppermute(value, 'col', [(i, i ^ bits) for i in range(count)])]
    unnamed x32 -> x30, local copies, waits for them, and re-layouts: 3.05 us -> 2.42 us
  transfers between devices with their start and end apart: 18 -> 18, of which waited for: 5 -> 3; matrix products, arithmetic and copies ran while one was open for 7% -> 7% of each run, Pallas kernels for 17% -> 23%
where the time goes in v3:
time: 147 us; the launch traced here: 146 us
  starting transfers between devices  57.5 us (39%)
  Pallas kernels  43.6 us (30%)
  waiting for transfers between devices  18.5 us (13%)
  blocking collectives  12.6 us (9%)
  local copies, waits for them, and re-layouts  7.68 us (5%)
  other arithmetic  3.54 us (2%)
    pallas_call x3, Pallas kernels, call(): pl.pallas_call(kernel, grid=(grid,), in_specs=[spec(entry, value.shape) f...  29.9 us
    ppermute x9, starting transfers between devices, swap(): return lax.ppermute(value, 'col', [(i, i ^ bits) for i in range(count)])  20.5 us
    all_to_all x3, starting transfers between devices, exchange(): return lax.all_to_all(value, 'gz', 0, 0, tiled=True)  19.9 us
    pallas_call x3, Pallas kernels, whole(): pl.pallas_call(kernel, in_specs=[spec(kind) for kind in ins], out_specs=t...  13.8 us
    all_to_all x1, blocking collectives, exchange(): return lax.all_to_all(value, 'gz', 0, 0, tiled=True)  12.6 us
    ppermute x1, waiting for transfers between devices, step(): g_low = lax.ppermute(gt_last, 'gz', up)  9.46 us
    all_to_all x3, waiting for transfers between devices, exchange(): return lax.all_to_all(value, 'gz', 0, 0, tiled=True)  8.97 us
    ppermute x1, starting transfers between devices, step(): back_from_high = lax.ppermute(back_low, 'gz', down)  5.44 us
  transfers between devices with their start and end apart: 18, of which 3 were waited for; matrix products, arithmetic and copies ran while one was open for 7% of the time, Pallas kernels for 23%

profile of v3, /device:TPU:1, one launch (start us, length us, event | category | flops | bytes accessed | tf_op | source)
XLA Modules:
  0.0 145.7 jit_solution(15514524551870895010)
XLA Ops:
  0.6 1.5 %collective-permute-start = (bf16[16,64,27]{1,0,2:T(8,128)(2,1)}, bf16[16,64,27]{1,0,2:T(8,128)(2,1)S(1)}, u32[]{:S(2)}, u32[]{:S(2)}) collective-permute-start(bf16[16,64,27]{1,0,2:T(8,128)(2,1)} %param.15), channel_id=1, source_target_pairs={{0,1},{1,0},{2,3},{3,2},{4,5},{5,4},{6,7},{7,6},{8,9},{9,8},{10,11... | collective-permute-start | bytes 165896 | tf_op jit(solution)/shard_map/ppermute | solution.py:487
  2.1 3.0 %collective-permute-start.1 = (bf16[16,64,27]{1,0,2:T(8,128)(2,1)}, bf16[16,64,27]{1,0,2:T(8,128)(2,1)S(1)}, u32[]{:S(2)}, u32[]{:S(2)}) collective-permute-start(bf16[16,64,27]{1,0,2:T(8,128)(2,1)} %param.15), channel_id=1, source_target_pairs={{0,2},{1,3},{2,0},{3,1},{4,6},{5,7},{6,4},{7,5},{8,10},{9,11},{10,... | collective-permute-start | bytes 165896 | tf_op jit(solution)/shard_map/ppermute | solution.py:487
  5.1 0.2 collective-permute-start.2
  5.3 0.7 copy-done.4
  6.0 0.7 copy-done.6
  6.7 3.7 %shard_map.157 = f32[256,128]{1,0:T(8,128)} custom-call(bf16[64,2,128,128]{3,2,1,0:T(8,128)(2,1)} %f_hbm.1, bf16[32,128]{1,0:T(8,128)(2,1)S(1)} %copy-done.4, bf16[16,256]{1,0:T(8,128)(2,1)S(1)} %copy-done.6), custom_call_target="tpu_custom_call" | custom-call | flops 1811939328 | bytes 8388608 | tf_op jit(solution)/shard_map/pallas_call | solution.py:69
  10.4 9.1 %all-to-all-start = ((f32[32,8,128]{2,1,0:T(8,128)}), f32[32,8,128]{2,1,0:T(8,128)S(1)}, u32[]{:S(2)}, u32[]{:S(2)}) async-start(f32[32,8,128]{2,1,0:T(8,128)} %bitcast.9), calls=%async_computation | async-start | bytes 262144 | tf_op jit(solution)/shard_map/all_to_all | solution.py:491
  19.7 0.8 reshape.61.w_ref
  20.4 11.7 %shard_map.156 = (bf16[2,128,64,128]{3,2,1,0:T(8,128)(2,1)}, bf16[16,2,128,128]{3,2,1,0:T(8,128)(2,1)}, bf16[16,128,128]{2,1,0:T(8,128)(2,1)}, bf16[16,128,128]{2,1,0:T(8,128)(2,1)}) custom-call(bf16[64,2,128,128]{3,2,1,0:T(8,128)(2,1)} %f_hbm.1, bf16[144,192]{1,0:T(8,128)(2,1)} %reshape.61.w_ref), custom_call_target="tpu_custom_call" | custom-call | flops 1811939328 | bytes 8388608 | tf_op jit(solution)/shard_map/pallas_call | solution.py:48
  32.2 1.3 collective-permute-start.3
  33.5 4.5 %collective-permute-start.4 = (bf16[16,128,128]{2,1,0:T(8,128)(2,1)}, bf16[16,128,128]{2,1,0:T(8,128)(2,1)S(1)}, u32[]{:S(2)}, u32[]{:S(2)}) collective-permute-start(bf16[16,128,128]{2,1,0:T(8,128)(2,1)} %get-tuple-element.29), channel_id=1, source_target_pairs={{0,124},{4,0},{8,4},{12,8},{16,12},{20,16},{24,20},{28,24},{32,28}... | collective-permute-start | bytes 1572872 | tf_op jit(solution)/shard_map/ppermute | solution.py:525
  37.9 0.2 reshape.65
  38.1 0.3 convolution_bitcast_fusion
  38.5 0.3 fusion.1
  39.0 0.2 fusion.5
  39.2 0.3 copy.36
  39.5 0.9 reshape.66
  40.4 3.9 %all-to-all-start.1 = ((f32[32,2,128]{2,1,0:T(2,128)}), f32[32,2,128]{2,1,0:T(2,128)S(1)}, u32[]{:S(2)}, u32[]{:S(2)}) async-start(f32[32,2,128]{2,1,0:T(2,128)} %reshape.66), calls=%async_computation.1 | async-start | bytes 65536 | tf_op jit(solution)/shard_map/all_to_all | solution.py:491
  44.3 0.2 dynamic-slice_maximum_fusion
  44.5 0.3 copy.32
  44.7 0.9 reshape.63.w_ref
  45.6 5.8 %all-to-all-done.1 = f32[32,2,128]{2,1,0:T(2,128)S(1)} async-done(((f32[32,2,128]{2,1,0:T(2,128)}), f32[32,2,128]{2,1,0:T(2,128)S(1)}, u32[]{:S(2)}, u32[]{:S(2)}) %all-to-all-start.1) | async-done | bytes 32800 | tf_op jit(solution)/shard_map/all_to_all | solution.py:491
  51.5 7.1 %shard_map.158 = (bf16[16,2,128,128]{3,2,1,0:T(8,128)(2,1)}, bf16[2,128,16,128]{3,2,1,0:T(8,128)(2,1)S(1)}, bf16[128,16,128]{2,1,0:T(8,128)(2,1)S(1)}, bf16[128,16,128]{2,1,0:T(8,128)(2,1)S(1)}, f32[64,128]{1,0:T(8,128)S(1)}) custom-call(bf16[16,2,128,128]{3,2,1,0:T(8,128)(2,1)} %get-tuple-element.27.int_hbm, bf16[16,2,128,128]{3,2,1,0:T(8,128)(2,1)} %go_hbm.1, ...), custom_call_target="tpu_custom_call" | custom-call | flops 1811939328 | bytes 8388608 | tf_op jit(solution)/shard_map/pallas_call | solution.py:69
  58.6 2.7 %collective-permute-start.6 = (bf16[2,128,16,128]{3,2,1,0:T(8,128)(2,1)S(1)}, bf16[2,128,16,128]{3,2,1,0:T(8,128)(2,1)}, u32[]{:S(2)}, u32[]{:S(2)}) collective-permute-start(bf16[2,128,16,128]{3,2,1,0:T(8,128)(2,1)S(1)} %get-tuple-element.31.gt_ref.g0), channel_id=1, source_target_pairs={{0,2},{1,3},{2,0},{3,1},{4,6},{5,7},{6,4},{7,5},{8,10},{9,11},{10,... | collective-permute-start | bytes 3145736 | tf_op jit(solution)/shard_map/ppermute | solution.py:487
  61.3 0.3 collective-permute-start.7
  61.6 5.4 %collective-permute-start.8 = (bf16[128,16,128]{2,1,0:T(8,128)(2,1)S(1)}, bf16[128,16,128]{2,1,0:T(8,128)(2,1)S(1)}, u32[]{:S(2)}, u32[]{:S(2)}) collective-permute-start(bf16[128,16,128]{2,1,0:T(8,128)(2,1)S(1)} %get-tuple-element.35), channel_id=1, source_target_pairs={{0,124},{4,0},{8,4},{12,8},{16,12},{20,16},{24,20},{28,24},{32,28}... | collective-permute-start | bytes 1572872 | tf_op jit(solution)/shard_map/ppermute | solution.py:538
  67.0 9.5 %collective-permute-done.7.gl_ref = bf16[128,16,128]{2,1,0:T(8,128)(2,1)S(1)} collective-permute-done((bf16[128,16,128]{2,1,0:T(8,128)(2,1)S(1)}, bf16[128,16,128]{2,1,0:T(8,128)(2,1)S(1)}, u32[]{:S(2)}, u32[]{:S(2)}) %collective-permute-start.7) | collective-permute-done | bytes 524320 | tf_op jit(solution)/shard_map/ppermute | solution.py:537
  76.5 0.8 copy-done.13
  77.3 0.2 copy-done.14
  77.4 9.6 %shard_map.159 = bf16[256,128]{1,0:T(8,128)(2,1)} custom-call(bf16[2,128,64,128]{3,2,1,0:T(8,128)(2,1)} %get-tuple-element.33.xt_ref, bf16[2,128,16,128]{3,2,1,0:T(8,128)(2,1)} %copy-done, bf16[128,16,128]{2,1,0:T(8,128)(2,1)} %copy-done.13, bf16[128,16,128]{2,1,0:T(8,128)(2,1)} %copy-done.14), custom_call_target="tpu_custom_call" | custom-call | flops 1811939328 | bytes 8388608 | tf_op jit(solution)/shard_map/pallas_call | solution.py:48
  87.1 1.5 %pad_maximum_fusion = bf16[32,10,128]{2,1,0:T(8,128)(2,1)} fusion(bf16[32,8,128]{2,1,0:T(8,128)(2,1)} %bitcast.59, bf16[32,2,128]{2,1,0:T(2,128)(2,1)S(1)} %bitcast.60), kind=kLoop, calls=%fused_computation.14 | loop fusion | flops 163840 | bytes 163840 | tf_op jit(solution)/shard_map/concatenate | solution.py:543
  88.6 6.9 %all-to-all-start.2 = ((bf16[32,10,128]{2,1,0:T(8,128)(2,1)}), bf16[32,10,128]{2,1,0:T(8,128)(2,1)S(1)}, u32[]{:S(2)}, u32[]{:S(2)}) async-start(bf16[32,10,128]{2,1,0:T(8,128)(2,1)} %pad_maximum_fusion), calls=%async_computation.2 | async-start | bytes 262144 | tf_op jit(solution)/shard_map/all_to_all | solution.py:491
  95.5 4.1 %collective-permute-start.5 = (bf16[2,128,16,128]{3,2,1,0:T(8,128)(2,1)}, bf16[2,128,16,128]{3,2,1,0:T(8,128)(2,1)}, u32[]{:S(2)}, u32[]{:S(2)}) collective-permute-start(bf16[2,128,16,128]{3,2,1,0:T(8,128)(2,1)} %copy-done), channel_id=1, source_target_pairs={{0,1},{1,0},{2,3},{3,2},{4,5},{5,4},{6,7},{7,6},{8,9},{9,8},{10,11... | collective-permute-start | bytes 3145736 | tf_op jit(solution)/shard_map/ppermute | solution.py:487
  99.7 3.2 %all-to-all-done.2 = bf16[32,10,128]{2,1,0:T(8,128)(2,1)S(1)} async-done(((bf16[32,10,128]{2,1,0:T(8,128)(2,1)}), bf16[32,10,128]{2,1,0:T(8,128)(2,1)S(1)}, u32[]{:S(2)}, u32[]{:S(2)}) %all-to-all-start.2) | async-done | bytes 81952 | tf_op jit(solution)/shard_map/all_to_all | solution.py:491
  102.9 5.2 %collective-permute-start.9 = (bf16[2,128,16,128]{3,2,1,0:T(8,128)(2,1)}, bf16[2,128,16,128]{3,2,1,0:T(8,128)(2,1)}, u32[]{:S(2)}, u32[]{:S(2)}) collective-permute-start(bf16[2,128,16,128]{3,2,1,0:T(8,128)(2,1)} %collective-permute-done.6.g2), channel_id=1, source_target_pairs={{0,1},{1,0},{2,3},{3,2},{4,5},{5,4},{6,7},{7,6},{8,9},{9,8},{10,11... | collective-permute-start | bytes 3145736 | tf_op jit(solution)/shard_map/ppermute | solution.py:487
  108.2 0.2 fusion.6
  108.5 1.3 broadcast_multiply_fusion
  110.1 0.4 collective-permute-start.11
  110.5 3.2 %collective-permute-start.12 = (f32[16,16,8]{0,2,1:T(8,128)S(1)}, f32[16,16,8]{0,2,1:T(8,128)S(1)}, u32[]{:S(2)}, u32[]{:S(2)}) collective-permute-start(f32[16,16,8]{0,2,1:T(8,128)S(1)} %get-tuple-element.50), channel_id=1, source_target_pairs={{0,3},{1,2},{2,1},{3,0},{4,7},{5,6},{6,5},{7,4},{8,11},{9,10},{10,... | collective-permute-start | bytes 24584 | tf_op jit(solution)/shard_map/ppermute | solution.py:487
  113.8 8.5 %shard_map.160 = (bf16[16,2,128,128]{3,2,1,0:T(8,128)(2,1)}, bf16[16,128,128]{2,1,0:T(8,128)(2,1)}, bf16[16,128,128]{2,1,0:T(8,128)(2,1)}) custom-call(bf16[2,128,16,128]{3,2,1,0:T(8,128)(2,1)} %copy-done, bf16[2,128,16,128]{3,2,1,0:T(8,128)(2,1)} %collective-permute-done.5.g1, bf16[2,128,16,128]{3,2,1,0:T(8,128)(2,1)} %collective-permute-done.6.g2, ...), custom_call_target="tpu_custom_call" | custom-call | flops 1811939328 | bytes 8388608 | tf_op jit(solution)/shard_map/pallas_call | solution.py:48
  122.4 0.3 collective-permute-start.13
  122.7 5.4 %collective-permute-start.14 = (bf16[16,128,128]{2,1,0:T(8,128)(2,1)}, bf16[16,128,128]{2,1,0:T(8,128)(2,1)S(1)}, u32[]{:S(2)}, u32[]{:S(2)}) collective-permute-start(bf16[16,128,128]{2,1,0:T(8,128)(2,1)} %get-tuple-element.43), channel_id=1, source_target_pairs={{0,124},{4,0},{8,4},{12,8},{16,12},{20,16},{24,20},{28,24},{32,28}... | collective-permute-start | bytes 1572872 | tf_op jit(solution)/shard_map/ppermute | solution.py:562
  128.1 0.3 fusion
  128.4 0.3 copy.40
  128.7 0.2 convert_element_type.28
  129.0 12.6 %all_to_all.20 = bf16[32,10,128]{2,1,0:T(8,128)(2,1)S(1)} all-to-all(bf16[32,10,128]{2,1,0:T(8,128)(2,1)S(1)} %pad_maximum_fusion.1), channel_id=1, replica_groups=mesh['gz'=32,'col'=4] {'gz'}, dimensions={0} | all-to-all | bytes 163840 | tf_op jit(solution)/shard_map/all_to_all | solution.py:491
  141.9 0.7 copy.51
  142.6 3.0 %shard_map.161 = bf16[16,2,128,128]{3,2,1,0:T(8,128)(2,1)} custom-call(bf16[16,2,128,128]{3,2,1,0:T(8,128)(2,1)} %get-tuple-element.38.int_hbm, bf16[16,128,128]{2,1,0:T(8,128)(2,1)S(1)} %collective-permute-done.13.fl_ref, bf16[16,128,128]{2,1,0:T(8,128)(2,1)S(1)} %collective-permute-done.14.fh_ref, f32[64,128]{1,0:T(8,128)S(1)} %convert.4.s_ref, ...), custom_call_target="tpu_custom_call" | custom-call | flops 1811939328 | bytes 8388608 | tf_op jit(solution)/shard_map/pallas_call | solution.py:69
  (59 shorter events, 1.1 us)
Async XLA Ops:
  0.6 43.6 %collective-permute-start = (bf16[16,64,27]{1,0,2:T(8,128)(2,1)}, bf16[16,64,27]{1,0,2:T(8,128)(2,1)S(1)}, u32[]{:S(2)}, u32[]{:S(2)}) collective-permute-start(bf16[16,64,27]{1,0,2:T(8,128)(2,1)} %param.15), channel_id=1, source_target_pairs={{0,1},{1,0},{2,3},{3,2},{4,5},{5,4},{6,7},{7,6},{8,9},{9,8},{10,11... | collective-permute-start | bytes 165896 | tf_op jit(solution)/shard_map/ppermute | solution.py:487
  2.1 42.1 %collective-permute-start.1 = (bf16[16,64,27]{1,0,2:T(8,128)(2,1)}, bf16[16,64,27]{1,0,2:T(8,128)(2,1)S(1)}, u32[]{:S(2)}, u32[]{:S(2)}) collective-permute-start(bf16[16,64,27]{1,0,2:T(8,128)(2,1)} %param.15), channel_id=1, source_target_pairs={{0,2},{1,3},{2,0},{3,1},{4,6},{5,7},{6,4},{7,5},{8,10},{9,11},{10,... | collective-permute-start | bytes 165896 | tf_op jit(solution)/shard_map/ppermute | solution.py:487
  5.1 39.1 %collective-permute-start.2 = (bf16[16,64,27]{1,0,2:T(8,128)(2,1)}, bf16[16,64,27]{1,0,2:T(8,128)(2,1)S(1)}, u32[]{:S(2)}, u32[]{:S(2)}) collective-permute-start(bf16[16,64,27]{1,0,2:T(8,128)(2,1)} %param.15), channel_id=1, source_target_pairs={{0,3},{1,2},{2,1},{3,0},{4,7},{5,6},{6,5},{7,4},{8,11},{9,10},{10,... | collective-permute-start | bytes 165896 | tf_op jit(solution)/shard_map/ppermute | solution.py:487
  5.3 0.7 copy-start.4
  6.0 0.7 copy-start.6
  6.7 12.9 %copy-start.9 = (bf16[16,64,27]{1,0,2:T(8,128)(2,1)S(1)}, bf16[16,64,27]{1,0,2:T(8,128)(2,1)}, u32[]{:S(2)}) copy-start(bf16[16,64,27]{1,0,2:T(8,128)(2,1)} %param.15) | copy-start | bytes 165892
  10.4 27.7 %copy-start.12 = (f32[16,32,2,1]{1,0,2,3:T(8,128)S(1)}, f32[16,32,2,1]{1,0,2,3:T(8,128)}, u32[]{:S(2)}) copy-start(f32[16,32,2,1]{1,0,2,3:T(8,128)} %constant.45) | copy-start | bytes 12292
  10.4 28.1 %copy-start.8 = (bf16[64,16,16,8]{0,3,2,1:T(8,128)(2,1)S(1)}, bf16[64,16,16,8]{0,3,2,1:T(8,128)(2,1)}, u32[]{:S(2)}) copy-start(bf16[64,16,16,8]{0,3,2,1:T(8,128)(2,1)} %param.16) | copy-start | bytes 786436
  10.4 27.5 %all-to-all-start = ((f32[32,8,128]{2,1,0:T(8,128)}), f32[32,8,128]{2,1,0:T(8,128)S(1)}, u32[]{:S(2)}, u32[]{:S(2)}) async-start(f32[32,8,128]{2,1,0:T(8,128)} %bitcast.9), calls=%async_computation | async-start | bytes 262144 | tf_op jit(solution)/shard_map/all_to_all | solution.py:491
  20.4 18.5 %copy-start.10 = (f32[16,64,1]{1,0,2:T(8,128)S(1)}, f32[16,64,1]{1,0,2:T(8,128)}, u32[]{:S(2)}) copy-start(f32[16,64,1]{1,0,2:T(8,128)} %constant.44) | copy-start | bytes 12292
  32.1 19.3 %copy-start.1 = (bf16[256,128]{1,0:T(8,128)(2,1)S(1)}, bf16[256,128]{1,0:T(8,128)(2,1)}, u32[]{:S(2)}) copy-start(bf16[256,128]{1,0:T(8,128)(2,1)} %constant.39.clone.eyh_ref) | copy-start | bytes 196612
  32.1 19.3 %copy-start.2 = (bf16[256,128]{1,0:T(8,128)(2,1)S(1)}, bf16[256,128]{1,0:T(8,128)(2,1)}, u32[]{:S(2)}) copy-start(bf16[256,128]{1,0:T(8,128)(2,1)} %constant.40.clone.eyl_ref) | copy-start | bytes 196612
  32.1 19.3 %copy-start.3 = (bf16[128,48]{1,0:T(8,128)(2,1)S(1)}, bf16[128,48]{1,0:T(8,128)(2,1)}, u32[]{:S(2)}) copy-start(bf16[128,48]{1,0:T(8,128)(2,1)} %constant.38.clone.ext3_ref) | copy-start | bytes 36868
  32.1 19.3 %copy-start.5 = (bf16[32,128]{1,0:T(8,128)(2,1)S(1)}, bf16[32,128]{1,0:T(8,128)(2,1)}, u32[]{:S(2)}) copy-start(bf16[32,128]{1,0:T(8,128)(2,1)} %constant.34.clone.ex2_ref) | copy-start | bytes 24580
  32.1 19.3 %copy-start.7 = (bf16[16,256]{1,0:T(8,128)(2,1)S(1)}, bf16[16,256]{1,0:T(8,128)(2,1)}, u32[]{:S(2)}) copy-start(bf16[16,256]{1,0:T(8,128)(2,1)} %constant.35.clone.ey2_ref) | copy-start | bytes 24580
  32.2 19.2 %collective-permute-start.3 = (bf16[16,128,128]{2,1,0:T(8,128)(2,1)}, bf16[16,128,128]{2,1,0:T(8,128)(2,1)S(1)}, u32[]{:S(2)}, u32[]{:S(2)}) collective-permute-start(bf16[16,128,128]{2,1,0:T(8,128)(2,1)} %get-tuple-element.28), channel_id=1, source_target_pairs={{0,4},{4,8},{8,12},{12,16},{16,20},{20,24},{24,28},{28,32},{32,36}... | collective-permute-start | bytes 1572872 | tf_op jit(solution)/shard_map/ppermute | solution.py:524
  33.5 18.0 %collective-permute-start.4 = (bf16[16,128,128]{2,1,0:T(8,128)(2,1)}, bf16[16,128,128]{2,1,0:T(8,128)(2,1)S(1)}, u32[]{:S(2)}, u32[]{:S(2)}) collective-permute-start(bf16[16,128,128]{2,1,0:T(8,128)(2,1)} %get-tuple-element.29), channel_id=1, source_target_pairs={{0,124},{4,0},{8,4},{12,8},{16,12},{20,16},{24,20},{28,24},{32,28}... | collective-permute-start | bytes 1572872 | tf_op jit(solution)/shard_map/ppermute | solution.py:525
  40.4 11.0 %all-to-all-start.1 = ((f32[32,2,128]{2,1,0:T(2,128)}), f32[32,2,128]{2,1,0:T(2,128)S(1)}, u32[]{:S(2)}, u32[]{:S(2)}) async-start(f32[32,2,128]{2,1,0:T(2,128)} %reshape.66), calls=%async_computation.1 | async-start | bytes 65536 | tf_op jit(solution)/shard_map/all_to_all | solution.py:491
  58.6 17.9 %copy-start = (bf16[2,128,16,128]{3,2,1,0:T(8,128)(2,1)}, bf16[2,128,16,128]{3,2,1,0:T(8,128)(2,1)S(1)}, u32[]{:S(2)}) copy-start(bf16[2,128,16,128]{3,2,1,0:T(8,128)(2,1)S(1)} %get-tuple-element.31.gt_ref.g0) | copy-start | bytes 3145732
  58.6 49.6 %copy-start.11 = (f32[16,32,2,1,1]{1,0,2,4,3:T(8,128)S(1)}, f32[16,32,2,1,1]{1,0,2,4,3:T(8,128)}, u32[]{:S(2)}) copy-start(f32[16,32,2,1,1]{1,0,2,4,3:T(8,128)} %constant.46) | copy-start | bytes 12292
  58.6 44.2 %collective-permute-start.6 = (bf16[2,128,16,128]{3,2,1,0:T(8,128)(2,1)S(1)}, bf16[2,128,16,128]{3,2,1,0:T(8,128)(2,1)}, u32[]{:S(2)}, u32[]{:S(2)}) collective-permute-start(bf16[2,128,16,128]{3,2,1,0:T(8,128)(2,1)S(1)} %get-tuple-element.31.gt_ref.g0), channel_id=1, source_target_pairs={{0,2},{1,3},{2,0},{3,1},{4,6},{5,7},{6,4},{7,5},{8,10},{9,11},{10,... | collective-permute-start | bytes 3145736 | tf_op jit(solution)/shard_map/ppermute | solution.py:487
  61.3 15.2 %collective-permute-start.7 = (bf16[128,16,128]{2,1,0:T(8,128)(2,1)S(1)}, bf16[128,16,128]{2,1,0:T(8,128)(2,1)S(1)}, u32[]{:S(2)}, u32[]{:S(2)}) collective-permute-start(bf16[128,16,128]{2,1,0:T(8,128)(2,1)S(1)} %get-tuple-element.34), channel_id=1, source_target_pairs={{0,4},{4,8},{8,12},{12,16},{16,20},{20,24},{24,28},{28,32},{32,36}... | collective-permute-start | bytes 1572872 | tf_op jit(solution)/shard_map/ppermute | solution.py:537
  61.6 14.9 %collective-permute-start.8 = (bf16[128,16,128]{2,1,0:T(8,128)(2,1)S(1)}, bf16[128,16,128]{2,1,0:T(8,128)(2,1)S(1)}, u32[]{:S(2)}, u32[]{:S(2)}) collective-permute-start(bf16[128,16,128]{2,1,0:T(8,128)(2,1)S(1)} %get-tuple-element.35), channel_id=1, source_target_pairs={{0,124},{4,0},{8,4},{12,8},{16,12},{20,16},{24,20},{28,24},{32,28}... | collective-permute-start | bytes 1572872 | tf_op jit(solution)/shard_map/ppermute | solution.py:538
  76.5 0.8 copy-start.13
  76.5 1.0 copy-start.14
  88.6 14.2 %all-to-all-start.2 = ((bf16[32,10,128]{2,1,0:T(8,128)(2,1)}), bf16[32,10,128]{2,1,0:T(8,128)(2,1)S(1)}, u32[]{:S(2)}, u32[]{:S(2)}) async-start(bf16[32,10,128]{2,1,0:T(8,128)(2,1)} %pad_maximum_fusion), calls=%async_computation.2 | async-start | bytes 262144 | tf_op jit(solution)/shard_map/all_to_all | solution.py:491
  95.5 18.2 %collective-permute-start.5 = (bf16[2,128,16,128]{3,2,1,0:T(8,128)(2,1)}, bf16[2,128,16,128]{3,2,1,0:T(8,128)(2,1)}, u32[]{:S(2)}, u32[]{:S(2)}) collective-permute-start(bf16[2,128,16,128]{3,2,1,0:T(8,128)(2,1)} %copy-done), channel_id=1, source_target_pairs={{0,1},{1,0},{2,3},{3,2},{4,5},{5,4},{6,7},{7,6},{8,9},{9,8},{10,11... | collective-permute-start | bytes 3145736 | tf_op jit(solution)/shard_map/ppermute | solution.py:487
  102.9 10.9 %collective-permute-start.9 = (bf16[2,128,16,128]{3,2,1,0:T(8,128)(2,1)}, bf16[2,128,16,128]{3,2,1,0:T(8,128)(2,1)}, u32[]{:S(2)}, u32[]{:S(2)}) collective-permute-start(bf16[2,128,16,128]{3,2,1,0:T(8,128)(2,1)} %collective-permute-done.6.g2), channel_id=1, source_target_pairs={{0,1},{1,0},{2,3},{3,2},{4,5},{5,4},{6,7},{7,6},{8,9},{9,8},{10,11... | collective-permute-start | bytes 3145736 | tf_op jit(solution)/shard_map/ppermute | solution.py:487
  110.0 12.4 %collective-permute-start.10 = (f32[16,16,8]{0,2,1:T(8,128)S(1)}, f32[16,16,8]{0,2,1:T(8,128)S(1)}, u32[]{:S(2)}, u32[]{:S(2)}) collective-permute-start(f32[16,16,8]{0,2,1:T(8,128)S(1)} %get-tuple-element.52), channel_id=1, source_target_pairs={{0,1},{1,0},{2,3},{3,2},{4,5},{5,4},{6,7},{7,6},{8,9},{9,8},{10,11... | collective-permute-start | bytes 24584 | tf_op jit(solution)/shard_map/ppermute | solution.py:487
  110.1 12.3 %collective-permute-start.11 = (f32[16,16,8]{0,2,1:T(8,128)S(1)}, f32[16,16,8]{0,2,1:T(8,128)S(1)}, u32[]{:S(2)}, u32[]{:S(2)}) collective-permute-start(f32[16,16,8]{0,2,1:T(8,128)S(1)} %get-tuple-element.51), channel_id=1, source_target_pairs={{0,2},{1,3},{2,0},{3,1},{4,6},{5,7},{6,4},{7,5},{8,10},{9,11},{10,... | collective-permute-start | bytes 24584 | tf_op jit(solution)/shard_map/ppermute | solution.py:487
  110.5 11.9 %collective-permute-start.12 = (f32[16,16,8]{0,2,1:T(8,128)S(1)}, f32[16,16,8]{0,2,1:T(8,128)S(1)}, u32[]{:S(2)}, u32[]{:S(2)}) collective-permute-start(f32[16,16,8]{0,2,1:T(8,128)S(1)} %get-tuple-element.50), channel_id=1, source_target_pairs={{0,3},{1,2},{2,1},{3,0},{4,7},{5,6},{6,5},{7,4},{8,11},{9,10},{10,... | collective-permute-start | bytes 24584 | tf_op jit(solution)/shard_map/ppermute | solution.py:487
  122.4 20.2 %collective-permute-start.13 = (bf16[16,128,128]{2,1,0:T(8,128)(2,1)}, bf16[16,128,128]{2,1,0:T(8,128)(2,1)S(1)}, u32[]{:S(2)}, u32[]{:S(2)}) collective-permute-start(bf16[16,128,128]{2,1,0:T(8,128)(2,1)} %get-tuple-element.42), channel_id=1, source_target_pairs={{0,4},{4,8},{8,12},{12,16},{16,20},{20,24},{24,28},{28,32},{32,36}... | collective-permute-start | bytes 1572872 | tf_op jit(solution)/shard_map/ppermute | solution.py:561
  122.7 19.9 %collective-permute-start.14 = (bf16[16,128,128]{2,1,0:T(8,128)(2,1)}, bf16[16,128,128]{2,1,0:T(8,128)(2,1)S(1)}, u32[]{:S(2)}, u32[]{:S(2)}) collective-permute-start(bf16[16,128,128]{2,1,0:T(8,128)(2,1)} %get-tuple-element.43), channel_id=1, source_target_pairs={{0,124},{4,0},{8,4},{12,8},{16,12},{20,16},{24,20},{28,24},{32,28}... | collective-permute-start | bytes 1572872 | tf_op jit(solution)/shard_map/ppermute | solution.py:562
